TPU v7x, 32 devices: a whole 2x2x4 slice. The times are simulated.
32 devices in a mesh: grp: 2 (over x), gy: 16 (over z, y, core).
Axes of the slice: x: 2, y: 2, z: 4, core: 2. Of those that a mesh axis runs over, the one named last changes fastest.
Arguments:
- vectors: bfloat16 [512, 2, 3, 16, 512], P('grp', None, None, 'gy'), parts along dimension 0, may hold values from -6 to 6
- gauge_links: bfloat16 [4, 2, 3, 3, 16, 512], P('grp', None, None, None, 'gy'), parts along dimension 0, may hold values from -4 to 4
- perambulators: bfloat16 [32, 4, 2, 2, 256, 256], P('grp', None, None, None, 'gy'), parts along dimension 0, may hold values from -0.25 to 0.25
- momenta: int32 [4, 3], replicated, may hold values from -2 to 2
- path_codes: int32 [2, 2], replicated, may hold values from 0 to 1
- source_times: int32 [8], P('grp'), parts along dimension 0, may hold values from 0 to 15
Outputs:
- contracted: bfloat16 [8, 4, 2, 256, 2, 4, 2, 256], P('grp', None, None, 'gy'), parts along dimension 0
There are 2 independent parts, one for each index of `grp`. A program takes and returns all parts, laid end to end along the dimension named above; an argument that names none is the same for every part. Nothing has to cross between parts.
Inputs may be any that keep to these rules, and one draw needn't show every extreme that they name: `momenta`: momentum components in lattice units.
All inputs are finite; a program needn't handle non-finite values.
Results may differ from a plain program's by a relative error of at most 0.0057.
Values may be sent and summed in bfloat16 or wider, within the bound.
A program may use at most 128 MiB of HBM per device.

v0:
```python
import math

import jax
import jax.numpy as jnp
from jax import lax
from jax.sharding import PartitionSpec as P

LX = 32
LZ = 16


TWO_PI = 6.283185307179586


def extended(cells, sides, width):
    for axis, dim in sides:
        count = lax.axis_size(axis)
        head = lax.slice_in_dim(cells, 0, width, axis=dim)
        tail = lax.slice_in_dim(cells, cells.shape[dim] - width, cells.shape[dim], axis=dim)
        cells = jnp.concatenate(
            [
                lax.ppermute(tail, axis, [(i, (i + 1) % count) for i in range(count)]),
                cells,
                lax.ppermute(head, axis, [((i + 1) % count, i) for i in range(count)]),
            ],
            axis=dim,
        )
    return cells


def color_apply(link_re, link_im, source_re, source_im, dagger):
    if dagger:
        link_re = jnp.swapaxes(link_re, 0, 1)
        link_im = -jnp.swapaxes(link_im, 0, 1)
    real_part = (
        link_re[:, 0][None] * source_re[:, 0][:, None]
        - link_im[:, 0][None] * source_im[:, 0][:, None]
    )
    imag_part = (
        link_re[:, 0][None] * source_im[:, 0][:, None]
        + link_im[:, 0][None] * source_re[:, 0][:, None]
    )
    for column in range(1, 3):
        real_part = (
            real_part
            + link_re[:, column][None] * source_re[:, column][:, None]
            - link_im[:, column][None] * source_im[:, column][:, None]
        )
        imag_part = (
            imag_part
            + link_re[:, column][None] * source_im[:, column][:, None]
            + link_im[:, column][None] * source_re[:, column][:, None]
        )
    return jnp.stack([real_part, imag_part], axis=1)


def link_step(link_data, source_field, dagger):
    return color_apply(
        link_data[0].astype(jnp.float32),
        link_data[1].astype(jnp.float32),
        source_field[:, 0].astype(jnp.float32),
        source_field[:, 1].astype(jnp.float32),
        dagger,
    )


def z_step(links_z, source_field, code_value):

    def ahead(field):
        return color_apply(
            links_z[0],
            links_z[1],
            jnp.roll(field[:, 0], -LX, -1),
            jnp.roll(field[:, 1], -LX, -1),
            False,
        )

    def behind(field):
        return color_apply(
            jnp.roll(links_z[0], LX, -1),
            jnp.roll(links_z[1], LX, -1),
            jnp.roll(field[:, 0], LX, -1),
            jnp.roll(field[:, 1], LX, -1),
            True,
        )

    return lax.cond(code_value == 1, ahead, behind, source_field)


def phase_angles(momenta, y_coord, y_total):
    positions = jnp.arange(LZ * LX, dtype=jnp.int32)
    x_coord = positions % LX
    z_coord = positions // LX
    mom_x = momenta[:, 0][:, None, None]
    mom_y = momenta[:, 1][:, None, None]
    mom_z = momenta[:, 2][:, None, None]
    period = LX * y_total * LZ
    raw_phase = (
        mom_x * x_coord[None, None, :] * (y_total * LZ)
        + mom_y * y_coord[None, :, None] * (LX * LZ)
        + mom_z * z_coord[None, None, :] * (LX * y_total)
    )
    residue = jnp.mod(raw_phase, period)
    return residue.astype(jnp.float32) * (TWO_PI / period)


def phased_rows(source_field, angles):
    cosine = jnp.cos(angles)[:, None, None]
    sine_part = jnp.sin(angles)[:, None, None]
    real_in = source_field[None, :, 0]
    imag_in = source_field[None, :, 1]
    stacked = jnp.stack(
        [cosine * real_in + sine_part * imag_in, cosine * imag_in - sine_part * real_in], axis=2
    )
    return stacked.astype(jnp.bfloat16).reshape(angles.shape[0] * source_field.shape[0], -1)


def conj_rows(vectors):
    vec_count = vectors.shape[0]
    plain_rows = vectors.reshape(vec_count, -1)
    swapped = jnp.concatenate([-vectors[:, 1], vectors[:, 0]], axis=1).reshape(vec_count, -1)
    return jnp.concatenate([plain_rows, swapped], axis=0)


def fold_rows(block_rows, source_re, source_im):
    row_count = block_rows.shape[2]
    outputs = []
    for path_index in range(block_rows.shape[0]):
        real_part = block_rows[path_index, 0]
        imag_part = block_rows[path_index, 1]
        upper_rows = jnp.stack([real_part, imag_part], axis=2).reshape(row_count, -1)
        lower_rows = jnp.stack([-imag_part, real_part], axis=2).reshape(row_count, -1)
        outputs.append(
            jnp.dot(source_re, upper_rows, preferred_element_type=jnp.float32)
            + jnp.dot(source_im, lower_rows, preferred_element_type=jnp.float32)
        )
    return jnp.stack(outputs, axis=1)


def shards(vectors, gauge_links, perambulators, momenta, path_codes, source_times):
    vec_count = vectors.shape[0]
    y_rows = vectors.shape[3]
    site_count = vectors.shape[4]
    y_total = y_rows * lax.axis_size("gy")
    mom_count = momenta.shape[0]
    path_total = path_codes.shape[0]
    stacked = jnp.concatenate(
        [
            vectors.reshape(vec_count * 6, y_rows, site_count),
            gauge_links[0].reshape(18, y_rows, site_count),
        ],
        axis=0,
    )
    padded = extended(stacked, (("gy", 1),), 1)
    padded_vectors = padded[: vec_count * 6].reshape(vec_count, 2, 3, y_rows + 2, site_count)
    padded_links = padded[vec_count * 6 :].reshape(2, 3, 3, y_rows + 2, site_count)

    def y_ahead(operands):
        return link_step(operands[1][:, :, :, 1:-1], operands[0][:, :, :, 2:], False)

    def y_behind(operands):
        return link_step(operands[1][:, :, :, :-2], operands[0][:, :, :, :-2], True)

    links_z = gauge_links[1].astype(jnp.float32)
    y_coord = lax.axis_index("gy") * y_rows + jnp.arange(y_rows, dtype=jnp.int32)
    angles = phase_angles(momenta, y_coord, y_total)
    left_rows = conj_rows(vectors)
    norm_factor = 1.0 / math.sqrt(6 * y_total * site_count)
    chosen = perambulators[source_times]
    own_rows = perambulators.shape[4]
    source_re = chosen[:, :, :, 0].reshape(-1, vec_count)
    source_im = chosen[:, :, :, 1].reshape(-1, vec_count)
    partials = []
    for path_index in range(path_total):
        shifted = lax.cond(
            path_codes[path_index, 0] == 1, y_ahead, y_behind, (padded_vectors, padded_links)
        )
        shifted = z_step(links_z, shifted, path_codes[path_index, 1])
        right_rows = phased_rows(shifted, angles)
        product = lax.dot_general(
            left_rows, right_rows, (((1,), (1,)), ((), ())), preferred_element_type=jnp.float32
        )
        partial_value = product.reshape(2, vec_count, mom_count, vec_count)
        partials.append(partial_value)
    owned_rows = lax.psum_scatter(jnp.stack(partials), "gy", scatter_dimension=2, tiled=True)
    elemental = (owned_rows * norm_factor).astype(jnp.bfloat16)
    combined = fold_rows(lax.all_gather(elemental, "gy", axis=2, tiled=True), source_re, source_im)
    shaped = combined.reshape(chosen.shape[0], 4, 2, own_rows, path_total, mom_count, 2, vec_count)
    return shaped.astype(jnp.bfloat16)


def solution(mesh):
    placed = (
        P("grp", None, None, "gy", None),
        P("grp", None, None, None, "gy", None),
        P("grp", None, None, None, "gy", None),
        P(),
        P(),
        P("grp"),
    )
    return jax.shard_map(
        shards,
        mesh=mesh,
        in_specs=placed,
        out_specs=P("grp", None, None, "gy", None, None, None, None),
        check_vma=False,
    )
```

profile of v0, /device:TPU:0, one launch (start us, length us, event | category | flops | bytes accessed | tf_op | source)
XLA Modules:
  0.0 469.2 jit_solution(14642596451377757994)
XLA Ops:
  7.5 3.8 copy.53
  11.3 5.0 %reshape.1599 = bf16[1536,1,512]{2,0,1:T(8,128)(2,1)} reshape(bf16[256,2,3,1,512]{4,2,1,0,3:T(4,128)(2,1)} %copy.53) | data formatting | bytes 3145728 | tf_op jit(solution)/shard_map/reshape | solution.py:149
  16.3 2.8 constant_dynamic-update-slice_fusion.1
  20.2 5.0 %collective-permute-start.1 = (bf16[1554,1,512]{2,0,1:T(8,128)(2,1)}, bf16[1554,1,512]{2,0,1:T(8,128)(2,1)}, u32[]{:S(2)}, u32[]{:S(2)}) collective-permute-start(bf16[1554,1,512]{2,0,1:T(8,128)(2,1)} %constant_dynamic-update-slice_fusion), channel_id=1, source_target_pairs={{1,0},{2,1},{3,2},{4,3},{5,4},{6,5},{7,6},{8,7},{9,8},{10,9},{11,1... | collective-permute-start | bytes 4773896 | tf_op jit(solution)/shard_map/ppermute | solution.py:24
  25.2 3.4 fusion.70
  28.6 4.9 %copy.47 = bf16[256,2,3,1,512]{0,4,2,1,3:T(8,128)(2,1)} copy(bf16[256,2,3,1,512]{4,1,3,2,0:T(2,128)(2,1)} %param.14) | data formatting | bytes 3145728 | tf_op args[0]
  36.6 1.7 copy.341
  39.8 2.6 copy.50
  42.4 3.8 pad_maximum_fusion.22
  46.2 4.7 copy.51
  51.3 4.8 %pad_maximum_fusion.18 = bf16[1536,3,512]{2,0,1:T(8,128)(2,1)} fusion(bf16[1554,1,512]{2,0,1:T(8,128)(2,1)} %collective-permute-done.1, bf16[1554,1,512]{2,0,1:T(8,128)(2,1)} %constant_dynamic-update-slice_fusion, bf16[1554,1,512]{2,0,1:T(8,128)(2,1)} %collective-permute-done), kind=kLoop, calls=%fused_computation.229 | loop fusion | flops 14155776 | bytes 9492480 | tf_op jit(solution)/shard_map/concatenate | solution.py:20
  56.1 11.6 %reshape.1601 = bf16[256,2,3,3,512]{4,2,1,0,3:T(4,128)(2,1)} reshape(bf16[1536,3,512]{2,0,1:T(8,128)(2,1)} %pad_maximum_fusion.18) | data formatting | bytes 9437184 | tf_op jit(solution)/shard_map/reshape | solution.py:155
  68.5 42.5 %conditional.6 = (f32[256,2,3,1,512]{4,3,2,1,0:T(1,128)}) conditional(s32[]{:T(128)} %bitcast.80, (bf16[2,3,3,3,512]{4,3,2,1,0:T(4,128)(2,1)S(1)}, bf16[256,2,3,3,512]{4,2,1,0,3:T(4,128)(2,1)}) %tuple.208, (bf16[2,3,3,3,512]{4,3,2,1,0:T(4,128)(2,1)S(1)}, bf16[256,2,3,3,512]{4,2,1,0,3:T(4,128)(2,1)}) %tuple.209), branch_computations={%region_4.5_spmd, %region_5.6_spmd} | conditional | flops 10237440 | bytes 39561224 | solution.py:175
  76.3 11.9 %copy.65 = bf16[256,2,3,3,512]{4,3,2,1,0:T(4,128)(2,1)} copy(bf16[256,2,3,3,512]{4,2,1,0,3:T(4,128)(2,1)} %get-tuple-element.80) | data formatting | bytes 9437184 | tf_op jit(solution)/shard_map
  88.3 6.1 %fusion.16 = (f32[256,3,1,512]{3,2,1,0:T(1,128)S(1)}, f32[256,3,1,512]{3,2,1,0:T(1,128)S(1)}) fusion(bf16[256,2,3,3,512]{4,3,2,1,0:T(4,128)(2,1)} %copy.65), kind=kLoop, calls=%fused_computation.137 | loop fusion | flops 786432 | bytes 4718592 | tf_op jit(solution)/shard_map/cond/branch_1_fun/convert_element_type | solution.py:61
  94.4 2.4 fusion.60
  97.2 9.1 %multiply_subtract_fusion.5 = (f32[256,1,3,1,512]{4,3,2,1,0:T(1,128)S(1)}, f32[256,1,3,1,512]{4,3,2,1,0:T(1,128)S(1)}) fusion(f32[256,512]{1,0:T(8,128)S(1)} %bitcast.484, f32[3,512]{1,0:T(4,128)S(1)} %bitcast.505, f32[256,512]{1,0:T(8,128)S(1)} %bitcast.487, f32[3,512]{1,0:T(4,128)S(1)} %bitcast.509, f32[256,512]{1,0:T(8,128)S(1)} %bitcast.489, ...), kind=kLoop, calls=%fused_computation.139 | loop fusion | flops 8650752 | bytes 6328320 | tf_op jit(solution)/shard_map/cond/branch_1_fun/sub | solution.py:45
  106.3 4.4 pad_maximum_fusion.9
  111.0 35.0 %conditional.7 = (f32[256,2,3,1,512]{4,3,2,1,0:T(1,128)}) conditional(s32[]{:T(128)} %bitcast.78, (f32[2,3,3,1,512]{4,3,2,1,0:T(1,128)S(1)}, f32[256,2,3,1,512]{4,3,2,1,0:T(1,128)}) %tuple.31, (f32[2,3,3,1,512]{4,3,2,1,0:T(1,128)S(1)}, f32[256,2,3,1,512]{4,3,2,1,0:T(1,128)}) %tuple.31), branch_computations={%region_6.7_spmd, %region_7.8_spmd} | conditional | flops 10237440 | bytes 38006792 | solution.py:87
  111.0 4.1 slice_bitcast_fusion.17
  116.0 3.4 fusion.20
  120.3 3.4 fusion.18
  124.5 9.1 %multiply_subtract_fusion.6 = (f32[256,1,3,1,512]{4,3,2,1,0:T(1,128)S(1)}, f32[256,1,3,1,512]{4,3,2,1,0:T(1,128)S(1)}) fusion(f32[256,512]{1,0:T(8,128)S(1)} %get-tuple-element.257, f32[3,512]{1,0:T(4,128)S(1)} %get-tuple-element.259, f32[256,512]{1,0:T(8,128)S(1)} %get-tuple-element.261, f32[3,512]{1,0:T(4,128)S(1)} %get-tuple-element.263, ...), kind=kLoop, calls=%fused_computation.156 | loop fusion | flops 8650752 | bytes 6328320 | tf_op jit(solution)/shard_map/cond/branch_0_fun/sub | solution.py:45
  133.5 4.5 pad_maximum_fusion.10
  146.0 5.8 %fusion.69 = (f32[256,1,3,1,512]{4,3,2,1,0:T(1,128)}, f32[256,1,3,1,512]{4,3,2,1,0:T(1,128)}) fusion(f32[256,2,3,1,512]{4,3,2,1,0:T(1,128)} %get-tuple-element.333), kind=kLoop, calls=%fused_computation.310 | loop fusion | bytes 6291456 | tf_op jit(solution)/shard_map/slice | solution.py:110
  151.8 4.8 %copy.188 = f32[256,1,3,1,512]{0,4,2,1,3:T(8,128)} copy(f32[256,1,3,1,512]{4,3,2,1,0:T(1,128)} %get-tuple-element.302) | data formatting | bytes 3145728 | tf_op jit(solution)/shard_map/mul | solution.py:113
  156.6 4.8 %copy.189 = f32[256,1,3,1,512]{0,4,2,1,3:T(8,128)} copy(f32[256,1,3,1,512]{4,3,2,1,0:T(1,128)} %get-tuple-element.303) | data formatting | bytes 3145728 | tf_op jit(solution)/shard_map/mul | solution.py:113
  161.4 46.0 %conditional.4 = (f32[256,2,3,1,512]{4,3,2,1,0:T(1,128)}) conditional(s32[]{:T(128)} %bitcast.66, (bf16[2,3,3,3,512]{4,3,2,1,0:T(4,128)(2,1)S(1)}, bf16[256,2,3,3,512]{4,2,1,0,3:T(4,128)(2,1)}) %tuple.210, (bf16[2,3,3,3,512]{4,3,2,1,0:T(4,128)(2,1)S(1)}, bf16[256,2,3,3,512]{4,2,1,0,3:T(4,128)(2,1)}) %tuple.211), branch_computations={%region_0.1_spmd, %region_1.2_spmd} | conditional | flops 10237440 | bytes 39561224 | solution.py:175
  161.4 11.9 %copy.56 = bf16[256,2,3,3,512]{4,3,2,1,0:T(4,128)(2,1)} copy(bf16[256,2,3,3,512]{4,2,1,0,3:T(4,128)(2,1)} %get-tuple-element.74) | data formatting | bytes 9437184 | tf_op jit(solution)/shard_map
  173.3 4.5 fusion.1
  177.8 2.4 fusion.44
  180.6 9.1 %multiply_subtract_fusion = (f32[256,1,3,1,512]{4,3,2,1,0:T(1,128)S(1)}, f32[256,1,3,1,512]{4,3,2,1,0:T(1,128)S(1)}) fusion(f32[256,512]{1,0:T(8,128)S(1)} %bitcast.474, f32[3,512]{1,0:T(4,128)S(1)} %get-tuple-element.103, f32[256,512]{1,0:T(8,128)S(1)} %bitcast.476, f32[3,512]{1,0:T(4,128)S(1)} %get-tuple-element.105, f32[256,512]{1,0:T(8,128)S(1)} %bitcast.478, ...), kind=kLoop, calls=%fused_computation.7 | loop fusion | flops 8650752 | bytes 6328320 | tf_op jit(solution)/shard_map/cond/branch_0_fun/sub | solution.py:45
  189.7 4.4 pad_maximum_fusion
  207.4 41.2 %conditional.5 = (f32[256,2,3,1,512]{4,3,2,1,0:T(1,128)}) conditional(s32[]{:T(128)} %bitcast.64, (f32[2,3,3,1,512]{4,3,2,1,0:T(1,128)S(1)}, f32[256,2,3,1,512]{4,3,2,1,0:T(1,128)}) %tuple.30, (f32[2,3,3,1,512]{4,3,2,1,0:T(1,128)S(1)}, f32[256,2,3,1,512]{4,3,2,1,0:T(1,128)}) %tuple.30), branch_computations={%region_2.3_spmd, %region_3.4_spmd} | conditional | flops 10237440 | bytes 38006792 | solution.py:87
  218.9 4.1 slice_bitcast_fusion.9
  223.0 3.3 slice.727
  226.6 2.3 fusion.12
  228.9 3.3 slice.732
  232.4 2.3 fusion.10
  235.1 9.1 %multiply_subtract_fusion.3 = (f32[256,1,3,1,512]{4,3,2,1,0:T(1,128)S(1)}, f32[256,1,3,1,512]{4,3,2,1,0:T(1,128)S(1)}) fusion(f32[256,512]{1,0:T(8,128)S(1)} %get-tuple-element.184, f32[3,512]{1,0:T(4,128)S(1)} %bitcast.508, f32[256,512]{1,0:T(8,128)S(1)} %get-tuple-element.186, f32[3,512]{1,0:T(4,128)S(1)} %bitcast.512, ...), kind=kLoop, calls=%fused_computation.81 | loop fusion | flops 8650752 | bytes 6328320 | tf_op jit(solution)/shard_map/cond/branch_1_fun/sub | solution.py:45
  244.2 4.4 pad_maximum_fusion.5
  248.7 5.8 %fusion.68 = (f32[256,1,3,1,512]{4,3,2,1,0:T(1,128)}, f32[256,1,3,1,512]{4,3,2,1,0:T(1,128)}) fusion(f32[256,2,3,1,512]{4,3,2,1,0:T(1,128)} %get-tuple-element.331), kind=kLoop, calls=%fused_computation.309 | loop fusion | bytes 6291456 | tf_op jit(solution)/shard_map/slice | solution.py:110
  254.5 4.8 %copy.186 = f32[256,1,3,1,512]{0,4,2,1,3:T(8,128)} copy(f32[256,1,3,1,512]{4,3,2,1,0:T(1,128)} %get-tuple-element.300) | data formatting | bytes 3145728 | tf_op jit(solution)/shard_map/mul | solution.py:113
  259.3 4.8 %copy.187 = f32[256,1,3,1,512]{0,4,2,1,3:T(8,128)} copy(f32[256,1,3,1,512]{4,3,2,1,0:T(1,128)} %get-tuple-element.301) | data formatting | bytes 3145728 | tf_op jit(solution)/shard_map/mul | solution.py:113
  264.1 7.2 %fusion.26 = (bf16[4,256,1,3,1,512]{1,5,3,2,0,4:T(8,128)(2,1)S(1)}, bf16[4,256,1,3,1,512]{1,5,3,2,0,4:T(8,128)(2,1)S(1)}, bf16[4,256,1,3,1,512]{1,5,3,0,4,2:T(8,128)(2,1)S(1)}, bf16[4,256,1,3,1,512]{1,5,3,0,4,2:T(8,128)(2,1)}) fusion(f32[256,3,512]{0,2,1:T(8,128)} %bitcast.461, f32[4,512]{1,0:T(4,128)S(1)} %get-tuple-element.323, ...), kind=kLoop, calls=%fused_computation.235 | loop fusion | flops 25165824 | bytes 18890752 | tf_op jit(solution)/shard_map/stack | solution.py:112
  271.3 2.5 pad_maximum_fusion.17
  273.7 3.0 copy.70
  276.8 3.8 pad_maximum_fusion.16
  280.5 5.7 %convolution_bitcast_fusion.1 = f32[1,2,256,4,256]{4,2,3,1,0:T(8,128)S(1)} fusion(bf16[2,256,3072,1]{2,1,3,0:T(8,128)(2,1)S(1)} %bitcast.466, bf16[4,256,3072,1]{1,2,0,3:T(8,128)(2,1)} %bitcast.455), kind=kOutput, calls=%fused_computation.241 | convolution fusion | flops 3221225472 | bytes 11534336 | tf_op jit(solution)/shard_map/dot_general | solution.py:180
  286.3 3.4 convolution_bitcast_fusion
  289.7 2.4 pad_maximum_fusion.20
  292.4 81.4 %reduce-scatter.2.cloned.1.call-done = f32[2,2,16,4,256]{4,2,3,1,0:T(8,128)} async-done(((f32[2,2,256,4,256]{4,2,3,1,0:T(8,128)}), f32[2,2,16,4,256]{4,2,3,1,0:T(8,128)}) %reduce-scatter.2.cloned.1.call-update) | async-done | bytes 262160 | tf_op jit(solution)/shard_map/reduce_scatter | solution.py:185
  376.9 39.2 %all-gather.2.cloned.1.call-done = bf16[2,2,256,4,256]{4,2,3,1,0:T(8,128)(2,1)} async-done(((bf16[2,2,16,4,256]{4,2,3,1,0:T(8,128)(2,1)}), bf16[2,2,256,4,256]{4,2,3,1,0:T(8,128)(2,1)}) %all-gather.2.cloned.1.call-update) | async-done | bytes 2097168 | tf_op jit(solution)/shard_map/all_gather | solution.py:187
  416.1 2.8 slice_bitcast_fusion.27
  421.0 2.3 copy.72
  424.6 2.1 fusion.74
  426.6 2.1 add_convert_fusion.3
  428.7 4.5 stack.93
  433.2 2.7 pad_maximum_fusion.27
  435.8 2.3 copy.74
  438.1 4.0 fusion.75
  443.4 4.6 add_convert_fusion.2
  448.0 4.4 stack.96
  452.5 9.6 %pad_maximum_fusion.21 = bf16[4,4,2,16,2,4,2,256]{7,6,5,4,3,2,1,0:T(2,128)(2,1)} fusion(bf16[4,4,2,16,1,4,2,256]{7,6,5,4,3,2,1,0:T(2,128)(2,1)} %bitcast.447, bf16[4,4,2,16,1,4,2,256]{7,6,5,4,3,2,1,0:T(2,128)(2,1)} %bitcast.446), kind=kLoop, calls=%fused_computation.232 | loop fusion | flops 2097152 | bytes 8388608 | tf_op jit(solution)/shard_map/stack | solution.py:137
  (111 shorter events, 17.1 us)
Async XLA Ops:
  6.5 369.0 %copy-start = (bf16[16,4,2,2,16,256]{5,4,3,2,1,0:T(8,128)(2,1)S(1)}, bf16[16,4,2,2,16,256]{5,4,3,2,1,0:T(8,128)(2,1)}, u32[]{:S(2)}) copy-start(bf16[16,4,2,2,16,256]{5,4,3,2,1,0:T(8,128)(2,1)} %param.16) | copy-start | bytes 6291460
  6.5 367.3 %reduce-scatter.2.cloned.1.call-start = ((), (), s32[]{:S(2)}) async-start(), calls=%async_computation.1 | async-start | bytes 4456448 | tf_op jit(solution)/shard_map/reduce_scatter | solution.py:185
  16.3 8.9 %copy-start.1 = (bf16[256,2,3,1,512]{4,1,3,2,0:T(2,128)(2,1)S(1)}, bf16[256,2,3,1,512]{4,1,3,2,0:T(2,128)(2,1)}, u32[]{:S(2)}) copy-start(bf16[256,2,3,1,512]{4,1,3,2,0:T(2,128)(2,1)} %param.14) | copy-start | bytes 4718596
  19.7 31.5 %collective-permute-start = (bf16[1554,1,512]{2,0,1:T(8,128)(2,1)}, bf16[1554,1,512]{2,0,1:T(8,128)(2,1)}, u32[]{:S(2)}, u32[]{:S(2)}) collective-permute-start(bf16[1554,1,512]{2,0,1:T(8,128)(2,1)} %constant_dynamic-update-slice_fusion), channel_id=1, source_target_pairs={{0,1},{1,2},{2,3},{3,4},{4,5},{5,6},{6,7},{7,8},{8,9},{9,10},{10,1... | collective-permute-start | bytes 4773896 | tf_op jit(solution)/shard_map/ppermute | solution.py:22
  20.2 31.1 %collective-permute-start.1 = (bf16[1554,1,512]{2,0,1:T(8,128)(2,1)}, bf16[1554,1,512]{2,0,1:T(8,128)(2,1)}, u32[]{:S(2)}, u32[]{:S(2)}) collective-permute-start(bf16[1554,1,512]{2,0,1:T(8,128)(2,1)} %constant_dynamic-update-slice_fusion), channel_id=1, source_target_pairs={{1,0},{2,1},{3,2},{4,3},{5,4},{6,5},{7,6},{8,7},{9,8},{10,9},{11,1... | collective-permute-start | bytes 4773896 | tf_op jit(solution)/shard_map/ppermute | solution.py:24
  28.6 4.9 %copy-start.9 = (s32[2,2]{1,0:T(2,128)S(1)}, s32[2,2]{1,0:T(2,128)}, u32[]{:S(2)}) copy-start(s32[2,2]{1,0:T(2,128)} %param.18) | copy-start | bytes 52
  36.6 1.9 copy-start.2
  46.2 4.7 copy-start.8
  276.8 3.8 copy-start.5
  276.8 9.5 %slice-start = ((s8[6291456]{0:T(1024)(128)(4,1)}), s8[2097152]{0:T(1024)(128)(4,1)S(1)}, s32[]{:S(2)}) async-start(s8[6291456]{0:T(1024)(128)(4,1)} %bitcast.452), calls=%async_computation.3 | async-start | bytes 4194304
  280.5 5.7 %slice-start.1 = ((s8[6291456]{0:T(1024)(128)(4,1)}), s8[4194304]{0:T(1024)(128)(4,1)S(1)}, s32[]{:S(2)}) async-start(s8[6291456]{0:T(1024)(128)(4,1)} %bitcast.452), calls=%async_computation.4 | async-start | bytes 8388608
  292.1 83.3 %copy-start.10 = (s32[4]{0:T(128)S(1)}, s32[4]{0:T(128)}, u32[]{:S(2)}) copy-start(s32[4]{0:T(128)} %param.19) | copy-start | bytes 52
  292.1 124.0 %all-gather.2.cloned.1.call-start = ((), (), s32[]{:S(2)}) async-start(), calls=%async_computation.2 | async-start | bytes 2228224 | tf_op jit(solution)/shard_map/all_gather | solution.py:187
  416.1 2.8 copy-start.3
  424.6 2.1 copy-start.4
  424.6 2.1 copy-start.6
  442.1 1.3 copy-start.7
Sparse Core Ops, SparseCore 0:
  292.3 81.4 reduce-scatter.1
  376.0 40.1 all-gather.1
where the time goes:
time: 475 us; the launch traced here: 469 us
  local copies, waits for them, and re-layouts  144 us (30%)
  waiting for transfers between devices  121 us (25%)
  other arithmetic  119 us (25%)
  loops' own time  41.4 us (9%)
  matrix products  21.8 us (5%)
  between operations  16.3 us (3%)
  starting transfers between devices  5.73 us (1%)
    reduce_scatter x1, waiting for transfers between devices, shards(): lax.psum_scatter(jnp.stack(partials), 'gy', scatter_dimension=2, tiled=True)  81.4 us
    all_gather x1, waiting for transfers between devices, shards(): lax.all_gather(elemental, 'gy', axis=2, tiled=True)  39.2 us
    sub x4, other arithmetic, color_apply(): real_part + link_re[:, column][None] * source_re[:, column][:, None]  36.3 us
    another operation x2, local copies, waits for them, and re-layouts  23.9 us
    another operation x2, loops' own time, shards(): lax.cond(path_codes[path_index, 0] == 1, y_ahead, y_behind, (padded_vecto...  21.6 us
    another operation x2, loops' own time, z_step(): return lax.cond(code_value == 1, ahead, behind, source_field)  19.8 us
    another operation x4, other arithmetic, color_apply(): return jnp.stack([real_part, imag_part], axis=1)  17.7 us
    unnamed x30, local copies, waits for them, and re-layouts  13.4 us
  transfers between devices with their start and end apart: 4, of which 2 were waited for; matrix products, arithmetic and copies ran while one was open for 5% of the time, Pallas kernels for 0%

commit v1 on v0

v1 whole, which is shorter than its diff:
```python
import functools
import math

import jax
import jax.numpy as jnp
from jax import lax
from jax.experimental import pallas as pl
from jax.experimental.pallas import tpu as pltpu
from jax.sharding import PartitionSpec as P

LX = 32
LZ = 16
TWO_PI = 6.283185307179586
MESH = pl.DeviceIdType.MESH
BF = jnp.bfloat16
F32 = jnp.float32


def matmul3(a, b):
    re = jnp.sum(a[0][:, :, None] * b[0][None] - a[1][:, :, None] * b[1][None], axis=1)
    im = jnp.sum(a[0][:, :, None] * b[1][None] + a[1][:, :, None] * b[0][None], axis=1)
    return jnp.stack([re, im])


def dagger(a):
    t = jnp.swapaxes(a, 1, 2)
    return jnp.stack([t[0], -t[1]])


def path_link(link_y, link_z, link_z_up, code):
    forward_y = code[0] == 1
    step_y = jnp.where(forward_y, link_y, dagger(link_y))
    step_z = jnp.where(forward_y, link_z, link_z_up)
    ahead = matmul3(step_z, jnp.roll(step_y, -LX, -1))
    behind = jnp.roll(matmul3(dagger(step_z), step_y), LX, -1)
    return jnp.where(code[1] == 1, ahead, behind)


def phase_angles(momenta, y_coord, y_total):
    positions = jnp.arange(LZ * LX, dtype=jnp.int32)
    x_coord = positions % LX
    z_coord = positions // LX
    period = LX * y_total * LZ
    raw = (
        momenta[:, 0][:, None] * x_coord[None] * (y_total * LZ)
        + momenta[:, 1][:, None] * y_coord * (LX * LZ)
        + momenta[:, 2][:, None] * z_coord[None] * (LX * y_total)
    )
    return jnp.mod(raw, period).astype(F32) * (TWO_PI / period)


def elemental_kernel(codes, links, trig, here, above, out, both, left, rolled, right):
    d = pl.program_id(0)
    nv, width = left.shape[1], left.shape[2]
    sites = width // 6
    moms = right.shape[0]

    @pl.when(d == 0)
    def _():
        both[0] = here[...]
        both[1] = above[...]

    forward_y = codes[d, 0] == 1
    src = jnp.where(forward_y, 1, 0)
    shift = jnp.where(codes[d, 1] == 1, sites - LX, LX)
    rows = 16
    half = width // 2

    @pl.loop(0, nv // rows)
    def _(k):
        at = pl.ds(pl.multiple_of(k * rows, rows), rows)
        whole = both[1 - src, at, :]
        left[0, at, :] = whole
        left[1, at, :] = jnp.concatenate([-whole[:, half:], whole[:, :half]], axis=1)
        for c in range(6):
            piece = both[src, at, c * sites : (c + 1) * sites].astype(F32)
            rolled[at, c * sites : (c + 1) * sites] = pltpu.roll(piece, shift, 1)

    for lt in range(sites // 128):
        lanes = slice(lt * 128, (lt + 1) * 128)
        m = [jnp.broadcast_to(links[0, q : q + 1, lanes], (8, 128)) for q in range(18)]
        tr = [jnp.broadcast_to(trig[0, q : q + 1, lanes], (8, 128)) for q in range(2 * moms)]

        @pl.loop(0, nv // rows)
        def _(k):
            at = pl.ds(pl.multiple_of(k * rows, rows), rows)
            halves = []
            for h in range(2):
                sub = pl.ds(pl.multiple_of(k * rows + 8 * h, 8), 8)
                v = [rolled[sub, c * sites + lt * 128 : c * sites + (lt + 1) * 128] for c in range(6)]
                us = []
                for r in range(3):
                    re = m[3 * r] * v[0] - m[9 + 3 * r] * v[3]
                    im = m[3 * r] * v[3] + m[9 + 3 * r] * v[0]
                    for c in range(1, 3):
                        re = re + m[3 * r + c] * v[c] - m[9 + 3 * r + c] * v[3 + c]
                        im = im + m[3 * r + c] * v[3 + c] + m[9 + 3 * r + c] * v[c]
                    us.append((re, im))
                halves.append(us)
            for p in range(moms):
                for r in range(3):
                    res, ims = [], []
                    for h in range(2):
                        re, im = halves[h][r]
                        res.append(tr[p] * re + tr[moms + p] * im)
                        ims.append(tr[p] * im - tr[moms + p] * re)
                    off = r * sites + lt * 128
                    right[p, at, off : off + 128] = jnp.concatenate(res, axis=0).astype(BF)
                    off = off + half
                    right[p, at, off : off + 128] = jnp.concatenate(ims, axis=0).astype(BF)

    @pl.loop(0, moms)
    def _(p):
        cols = pl.ds(pl.multiple_of(p * nv, nv), nv)
        for c in range(2):
            out[0, c, :, cols] = lax.dot_general(
                left[c], right[p], (((1,), (1,)), ((), ())), preferred_element_type=F32
            ).astype(BF)


def exchange_kernel(chips, norm, partial, full, paired, send, landed, own, sems):
    me = lax.axis_index("gy")
    core = lax.rem(me, 2)
    chip = lax.div(me, 2)
    mate = me + 1 - 2 * core
    mate_core = 1 - core

    def chip_at(k):
        return lax.rem(chip + k, chips)

    barrier = pltpu.get_barrier_semaphore()
    pl.semaphore_signal(barrier, inc=1, device_id={"gy": mate}, device_id_type=MESH)
    for k in range(1, chips):
        pl.semaphore_signal(
            barrier, inc=1, device_id={"gy": 2 * chip_at(k) + core}, device_id_type=MESH
        )
    pl.semaphore_wait(barrier, chips)

    def remote(src, dst, kind, k, target):
        return pltpu.make_async_remote_copy(
            src_ref=src,
            dst_ref=dst,
            send_sem=sems.at[2 * kind, k],
            recv_sem=sems.at[2 * kind + 1, k],
            device_id={"gy": target},
            device_id_type=MESH,
        )

    order = list(range(1, chips)) + [0]
    pairs = []
    for k in order:
        c = chip_at(k)
        copy = remote(partial.at[:, :, 2 * c + mate_core], paired.at[k], 0, k, mate)
        copy.start()
        pairs.append(copy)
    outs = []
    for n, k in enumerate(order):
        pairs[n].wait_recv()
        c = chip_at(k)
        total = partial[:, :, 2 * c + core].astype(F32) + paired[k].astype(F32)
        if k == 0:
            own[...] = total
        else:
            send[k] = total.astype(BF)
            copy = remote(send.at[k], landed.at[k], 1, k, 2 * c + core)
            copy.start()
            outs.append(copy)
    for copy in outs:
        copy.wait_recv()
    total = own[...]
    for k in range(1, chips):
        total = total + landed[k].astype(F32)
    full[:, :, me] = (total * norm).astype(BF)

    gathers = []
    for k in range(1, chips):
        copy = remote(full.at[:, :, me], full.at[:, :, me], 2, k, 2 * chip_at(k) + core)
        copy.start()
        gathers.append(copy)
    copy = remote(full.at[:, :, me], full.at[:, :, me], 3, 0, mate)
    copy.start()
    relays = [copy]
    for k in range(1, chips):
        gathers[k - 1].wait_recv()
        origin = 2 * chip_at(chips - k) + core
        copy = remote(full.at[:, :, origin], full.at[:, :, origin], 3, k, mate)
        copy.start()
        relays.append(copy)
    for copy in relays:
        copy.wait_recv()
    for copy in pairs + outs + gathers + relays:
        copy.wait_send()


def contract_kernel(left, right, out):
    nv = out.shape[5]
    for d in range(out.shape[2]):
        for p in range(out.shape[3]):
            block = jnp.dot(
                left[0], right[d, :, p * nv : (p + 1) * nv], preferred_element_type=F32
            )
            out[0, :, d, p] = block.reshape(-1, 2, nv).astype(BF)


def shards(vectors, gauge_links, perambulators, momenta, path_codes, source_times):
    nv = vectors.shape[0]
    sites = vectors.shape[4]
    size = lax.axis_size("gy")
    y_total = vectors.shape[3] * size
    chips = size // 2
    moms = momenta.shape[0]
    paths = path_codes.shape[0]
    down = [((i + 1) % size, i) for i in range(size)]
    lead = jnp.transpose(vectors, (0, 2, 3, 1, 4))
    lead_up = lax.ppermute(lead, "gy", down)
    links_up = lax.ppermute(gauge_links[1], "gy", down)
    here = jnp.transpose(lead, (0, 3, 1, 2, 4)).reshape(nv, 6 * sites)
    above = jnp.transpose(lead_up, (0, 3, 1, 2, 4)).reshape(nv, 6 * sites)

    link_y = gauge_links[0, :, :, :, 0].astype(F32)
    link_z = gauge_links[1, :, :, :, 0].astype(F32)
    link_z_up = links_up[:, :, :, 0].astype(F32)
    y_here = lax.axis_index("gy")
    links, trig = [], []
    for d in range(paths):
        links.append(path_link(link_y, link_z, link_z_up, path_codes[d]))
        angles = phase_angles(momenta, y_here + jnp.where(path_codes[d, 0] == 1, 0, 1), y_total)
        trig.append(jnp.concatenate([jnp.cos(angles), jnp.sin(angles)]))
    links = jnp.stack(links).reshape(paths, 18, sites)
    trig = jnp.stack(trig)

    partial = pl.pallas_call(
        elemental_kernel,
        grid=(paths,),
        out_shape=jax.ShapeDtypeStruct((paths, 2, nv, moms * nv), BF),
        in_specs=[
            pl.BlockSpec(memory_space=pltpu.SMEM),
            pl.BlockSpec((1, 18, sites), lambda d: (d, 0, 0)),
            pl.BlockSpec((1, 2 * moms, sites), lambda d: (d, 0, 0)),
            pl.BlockSpec((nv, 6 * sites), lambda d: (0, 0)),
            pl.BlockSpec((nv, 6 * sites), lambda d: (0, 0)),
        ],
        out_specs=pl.BlockSpec((1, 2, nv, moms * nv), lambda d: (d, 0, 0, 0)),
        scratch_shapes=[
            pltpu.VMEM((2, nv, 6 * sites), BF),
            pltpu.VMEM((2, nv, 6 * sites), BF),
            pltpu.VMEM((nv, 6 * sites), F32),
            pltpu.VMEM((moms, nv, 6 * sites), BF),
        ],
        compiler_params=pltpu.CompilerParams(vmem_limit_bytes=60 * 2**20),
    )(path_codes, links, trig, here, above)

    rows = nv // size
    norm = 1.0 / math.sqrt(6 * y_total * sites)
    block = (paths, 2, rows, moms * nv)
    gathered = pl.pallas_call(
        functools.partial(exchange_kernel, chips, norm),
        out_shape=jax.ShapeDtypeStruct((paths, 2, size, rows, moms * nv), BF),
        in_specs=[pl.BlockSpec(memory_space=pltpu.VMEM)],
        out_specs=pl.BlockSpec(memory_space=pltpu.VMEM),
        scratch_shapes=[
            pltpu.VMEM((chips,) + block, BF),
            pltpu.VMEM((chips,) + block, BF),
            pltpu.VMEM((chips,) + block, BF),
            pltpu.VMEM(block, F32),
            pltpu.SemaphoreType.DMA((8, chips)),
        ],
        compiler_params=pltpu.CompilerParams(
            collective_id=0, has_side_effects=True, vmem_limit_bytes=60 * 2**20
        ),
    )(partial.reshape(paths, 2, size, rows, moms * nv))
    right = gathered.reshape(paths, 2 * nv, moms * nv)

    chosen = perambulators[source_times]
    times, spins, sources = chosen.shape[:3]
    own = chosen.shape[4]
    re, im = chosen[:, :, :, 0], chosen[:, :, :, 1]
    left = jnp.stack(
        [jnp.concatenate([re, -im], axis=-1), jnp.concatenate([im, re], axis=-1)], axis=4
    ).reshape(times, spins * sources * own * 2, 2 * nv)
    count = spins * sources * own
    out = pl.pallas_call(
        contract_kernel,
        grid=(times,),
        out_shape=jax.ShapeDtypeStruct((times, count, paths, moms, 2, nv), BF),
        in_specs=[
            pl.BlockSpec((1, 2 * count, 2 * nv), lambda s: (s, 0, 0)),
            pl.BlockSpec((paths, 2 * nv, moms * nv), lambda s: (0, 0, 0)),
        ],
        out_specs=pl.BlockSpec((1, count, paths, moms, 2, nv), lambda s: (s, 0, 0, 0, 0, 0)),
        compiler_params=pltpu.CompilerParams(vmem_limit_bytes=60 * 2**20),
    )(left, right)
    return out.reshape(times, spins, sources, own, paths, moms, 2, nv)


def solution(mesh):
    placed = (
        P("grp", None, None, "gy", None),
        P("grp", None, None, None, "gy", None),
        P("grp", None, None, None, "gy", None),
        P(),
        P(),
        P("grp"),
    )
    return jax.shard_map(
        shards,
        mesh=mesh,
        in_specs=placed,
        out_specs=P("grp", None, None, "gy", None, None, None, None),
        check_vma=False,
    )
```

time: 475 us -> 119 us (0.25)
  the two profiles are of different devices: /device:TPU:0 before, /device:TPU:31 now
where the time goes in v1:
time: 119 us
  Pallas kernels  86.1 us (72%)
  local copies, waits for them, and re-layouts  16.6 us (14%)
  waiting for transfers between devices  7.24 us (6%)
  other arithmetic  4.86 us (4%)
  between operations  3.13 us (3%)
    pallas_call x1, Pallas kernels, shards(): pl.pallas_call(functools.partial(exchange_kernel, chips, norm), out_shape...  57.6 us
    pallas_call x1, Pallas kernels, shards(): pl.pallas_call(elemental_kernel, grid=(paths,), out_shape=jax.ShapeDtypeS...  21.1 us
    pallas_call x1, Pallas kernels, shards(): pl.pallas_call(contract_kernel, grid=(times,), out_shape=jax.ShapeDtypeSt...  7.34 us
    ppermute x1, waiting for transfers between devices, shards(): lead_up = lax.ppermute(lead, 'gy', down)  7.23 us
    unnamed x33, local copies, waits for them, and re-layouts  5.25 us
    reshape x1, local copies, waits for them, and re-layouts, shards(): here = jnp.transpose(lead, (0, 3, 1, 2, 4)).reshape(nv, 6 * sites)  2.59 us
    reshape x1, local copies, waits for them, and re-layouts, shards(): above = jnp.transpose(lead_up, (0, 3, 1, 2, 4)).reshape(nv, 6 * sites)  2.58 us
  transfers between devices with their start and end apart: 2, of which 1 were waited for; matrix products, arithmetic and copies ran while one was open for 14% of the time, Pallas kernels for 0%

profile of v1, /device:TPU:31, one launch (start us, length us, event | category | flops | bytes accessed | tf_op | source)
XLA Modules:
  0.0 118.6 jit_solution(9635512587636015299)
XLA Ops:
  0.0 0.0 copy-start
  0.0 0.0 copy-start.1
  0.0 0.0 copy-start.7
  0.0 0.0 copy-start.10
  0.0 1.5 %slice_bitcast_fusion.2 = bf16[2,3,3,1,512]{4,0,2,1,3:T(2,128)(2,1)} fusion(bf16[2,2,3,3,1,512]{5,1,3,2,4,0:T(2,128)(2,1)} %bitcast.111), kind=kLoop, calls=%fused_computation.94 | loop fusion | bytes 36864 | tf_op jit(solution)/shard_map/squeeze | solution.py:216
  1.5 0.7 collective-permute-start
  2.2 4.9 %copy.41 = bf16[256,2,3,1,512]{0,4,2,1,3:T(8,128)(2,1)} copy(bf16[256,2,3,1,512]{4,1,3,2,0:T(2,128)(2,1)} %param.6) | data formatting | bytes 3145728 | tf_op args[0]
  7.1 0.0 collective-permute-start.1
  7.1 0.6 add_select_fusion.3
  7.6 0.6 add_select_fusion.2
  8.2 0.0 copy-done.1
  8.3 0.0 copy-done.7
  8.3 0.7 fusion.25
  10.2 0.1 broadcast_select_fusion.1
  10.3 0.1 slice.190
  10.4 0.1 slice.200
  10.5 0.7 fusion.19
  11.2 0.0 copy-done.10
  11.2 0.0 copy-done
  11.3 0.6 gather_fusion
  11.9 0.1 slice_bitcast_fusion
  11.9 0.1 fusion.1
  12.0 0.0 copy-start.6
  12.1 0.0 copy-start.8
  12.1 0.0 copy-start.9
  12.1 0.1 fusion
  12.2 0.0 copy-start.5
  12.2 0.0 copy-start.4
  12.2 0.0 copy-start.3
  12.2 0.0 copy-start.2
  12.3 0.1 maximum_bitcast_fusion
  12.4 0.1 pad_maximum_fusion
  12.5 0.2 copy-done.6
  12.7 0.2 multiply_reduce_fusion.1
  12.9 0.0 copy-done.8
  13.0 0.0 copy-done.9
  13.0 0.2 fusion.11
  13.2 0.6 pad_maximum_fusion.7.trig
  15.2 0.0 copy-done.5
  15.2 0.0 copy-done.4
  15.2 0.0 copy-done.3
  15.3 0.0 copy-done.2
  15.3 1.1 copy.32
  16.4 1.2 %reshape.171.left = bf16[4,256,512]{2,1,0:T(8,128)(2,1)} reshape(bf16[4,4,2,16,2,512]{5,4,3,2,1,0:T(2,128)(2,1)S(1)} %copy.32) | data formatting | bytes 2097152 | tf_op jit(solution)/shard_map/reshape | solution.py:280
  17.6 2.6 %copy.43.here = bf16[256,3072]{1,0:T(8,128)(2,1)} copy(bf16[256,3072]{0,1:T(8,128)(2,1)} %bitcast.100) | data formatting | bytes 3145728 | tf_op jit(solution)/shard_map/reshape | solution.py:217
  20.2 0.0 collective-permute-done
  20.2 0.8 convert_select_fusion.1
  21.0 0.1 subtract_reduce_fusion
  21.1 0.1 pad_maximum_fusion.10
  21.3 0.1 subtract_reduce_fusion.2
  21.4 0.1 pad_maximum_fusion.11
  21.5 0.1 fusion.20
  21.6 0.1 subtract_reduce_fusion.3
  21.7 0.1 subtract_reduce_fusion.1
  21.9 0.1 maximum_select_fusion
  21.9 0.1 maximum_select_fusion.1
  22.0 0.7 pad_maximum_fusion.1.links
  22.7 7.2 %collective-permute-done.1 = bf16[256,3,1,2,512]{0,4,1,3,2:T(8,128)(2,1)} collective-permute-done((bf16[256,3,1,2,512]{0,4,1,3,2:T(8,128)(2,1)}, bf16[256,3,1,2,512]{0,4,1,3,2:T(8,128)(2,1)}, u32[]{:S(2)}, u32[]{:S(2)}) %collective-permute-start.1) | collective-permute-done | bytes 1572896 | tf_op jit(solution)/shard_map/ppermute | solution.py:215
  29.9 2.6 %copy.44.above = bf16[256,3072]{1,0:T(8,128)(2,1)} copy(bf16[256,3072]{0,1:T(8,128)(2,1)} %bitcast.36) | data formatting | bytes 3145728 | tf_op jit(solution)/shard_map/reshape | solution.py:218
  32.5 21.1 %shard_map.64 = bf16[2,2,256,1024]{3,2,1,0:T(8,128)(2,1)} custom-call(s32[2,2]{1,0:T(2,128)} %codes.1, f32[2,18,512]{2,1,0:T(8,128)} %pad_maximum_fusion.1.links, f32[2,8,512]{2,1,0:T(8,128)} %pad_maximum_fusion.7.trig, bf16[256,3072]{1,0:T(8,128)(2,1)} %copy.43.here, bf16[256,3072]{1,0:T(8,128)(2,1)} %copy.44.above), custom_call_target="tpu_custom_call" | custom-call | tf_op jit(solution)/shard_map/pallas_call | solution.py:232
  53.7 57.6 %shard_map.65 = bf16[2,2,16,16,1024]{4,3,2,1,0:T(8,128)(2,1)} custom-call(bf16[2,2,16,16,1024]{4,3,2,1,0:T(8,128)(2,1)} %bitcast.98), custom_call_target="tpu_custom_call" | custom-call | tf_op jit(solution)/shard_map/pallas_call | solution.py:256
  111.3 7.3 %shard_map.66 = bf16[4,128,2,4,2,256]{5,4,3,2,1,0:T(2,128)(2,1)} custom-call(bf16[4,256,512]{2,1,0:T(8,128)(2,1)} %reshape.171.left, bf16[2,512,1024]{2,1,0:T(8,128)(2,1)} %bitcast.97), custom_call_target="tpu_custom_call" | custom-call | tf_op jit(solution)/shard_map/pallas_call | solution.py:282
  (32 shorter events, 0.5 us)
Async XLA Ops:
  0.0 11.2 %copy-start = (bf16[16,4,2,2,16,256]{5,4,3,2,1,0:T(8,128)(2,1)S(1)}, bf16[16,4,2,2,16,256]{5,4,3,2,1,0:T(8,128)(2,1)}, u32[]{:S(2)}) copy-start(bf16[16,4,2,2,16,256]{5,4,3,2,1,0:T(8,128)(2,1)} %param.8) | copy-start | bytes 6291460
  0.0 8.2 %copy-start.1 = (bf16[2,2,3,3,1,512]{5,1,4,3,2,0:T(2,128)(2,1)S(1)}, bf16[2,2,3,3,1,512]{5,1,4,3,2,0:T(2,128)(2,1)}, u32[]{:S(2)}) copy-start(bf16[2,2,3,3,1,512]{5,1,4,3,2,0:T(2,128)(2,1)} %param.7) | copy-start | bytes 110596
  0.0 8.2 %copy-start.7 = (s32[2,2]{1,0:T(2,128)S(1)}, s32[2,2]{1,0:T(2,128)}, u32[]{:S(2)}) copy-start(s32[2,2]{1,0:T(2,128)} %codes.1) | copy-start | bytes 52
  0.0 11.2 %copy-start.10 = (s32[4]{0:T(128)S(1)}, s32[4]{0:T(128)}, u32[]{:S(2)}) copy-start(s32[4]{0:T(128)} %param.11) | copy-start | bytes 52
  1.5 18.7 %collective-permute-start = (bf16[2,3,3,1,512]{4,0,2,1,3:T(2,128)(2,1)}, bf16[2,3,3,1,512]{4,0,2,1,3:T(2,128)(2,1)}, u32[]{:S(2)}, u32[]{:S(2)}) collective-permute-start(bf16[2,3,3,1,512]{4,0,2,1,3:T(2,128)(2,1)} %slice_bitcast_fusion.2), channel_id=1, source_target_pairs={{1,0},{2,1},{3,2},{4,3},{5,4},{6,5},{7,6},{8,7},{9,8},{10,9},{11,1... | collective-permute-start | bytes 55304 | tf_op jit(solution)/shard_map/ppermute | solution.py:216
  7.1 22.9 %collective-permute-start.1 = (bf16[256,3,1,2,512]{0,4,1,3,2:T(8,128)(2,1)}, bf16[256,3,1,2,512]{0,4,1,3,2:T(8,128)(2,1)}, u32[]{:S(2)}, u32[]{:S(2)}) collective-permute-start(bf16[256,3,1,2,512]{0,4,1,3,2:T(8,128)(2,1)} %bitcast.99), channel_id=1, source_target_pairs={{1,0},{2,1},{3,2},{4,3},{5,4},{6,5},{7,6},{8,7},{9,8},{10,9},{11,1... | collective-permute-start | bytes 4718600 | tf_op jit(solution)/shard_map/ppermute | solution.py:215
  12.0 0.7 copy-start.6
  12.1 0.9 copy-start.8
  12.1 0.9 copy-start.9
  12.2 3.0 %copy-start.5 = (f32[1,3,3,512]{3,0,2,1:T(1,128)S(1)}, f32[1,3,3,512]{3,0,2,1:T(1,128)}, u32[]{:S(2)}) copy-start(f32[1,3,3,512]{3,0,2,1:T(1,128)} %get-tuple-element.31) | copy-start | bytes 55300
  12.2 3.0 %copy-start.4 = (f32[1,3,3,512]{3,0,2,1:T(1,128)S(1)}, f32[1,3,3,512]{3,0,2,1:T(1,128)}, u32[]{:S(2)}) copy-start(f32[1,3,3,512]{3,0,2,1:T(1,128)} %get-tuple-element.32) | copy-start | bytes 55300
  12.2 3.0 %copy-start.3 = (f32[1,3,3,512]{3,0,2,1:T(1,128)S(1)}, f32[1,3,3,512]{3,0,2,1:T(1,128)}, u32[]{:S(2)}) copy-start(f32[1,3,3,512]{3,0,2,1:T(1,128)} %get-tuple-element.53) | copy-start | bytes 55300
  12.2 3.0 %copy-start.2 = (f32[1,3,3,512]{3,0,2,1:T(1,128)S(1)}, f32[1,3,3,512]{3,0,2,1:T(1,128)}, u32[]{:S(2)}) copy-start(f32[1,3,3,512]{3,0,2,1:T(1,128)} %get-tuple-element.54) | copy-start | bytes 55300

commit v2 on v1

v2 whole, which is shorter than its diff:
```python
import functools
import math

import jax
import jax.numpy as jnp
from jax import lax
from jax.experimental import pallas as pl
from jax.experimental.pallas import tpu as pltpu
from jax.sharding import PartitionSpec as P

LX = 32
LZ = 16
TWO_PI = 6.283185307179586
MESH = pl.DeviceIdType.MESH
BF = jnp.bfloat16
F32 = jnp.float32


def matmul3(a, b):
    re = jnp.sum(a[0][:, :, None] * b[0][None] - a[1][:, :, None] * b[1][None], axis=1)
    im = jnp.sum(a[0][:, :, None] * b[1][None] + a[1][:, :, None] * b[0][None], axis=1)
    return jnp.stack([re, im])


def dagger(a):
    t = jnp.swapaxes(a, 1, 2)
    return jnp.stack([t[0], -t[1]])


def path_link(link_y, link_z, link_z_up, code):
    forward_y = code[0] == 1
    step_y = jnp.where(forward_y, link_y, dagger(link_y))
    step_z = jnp.where(forward_y, link_z, link_z_up)
    ahead = matmul3(step_z, jnp.roll(step_y, -LX, -1))
    behind = jnp.roll(matmul3(dagger(step_z), step_y), LX, -1)
    return jnp.where(code[1] == 1, ahead, behind)


def phase_angles(momenta, y_coord, y_total):
    positions = jnp.arange(LZ * LX, dtype=jnp.int32)
    x_coord = positions % LX
    z_coord = positions // LX
    period = LX * y_total * LZ
    raw = (
        momenta[:, 0][:, None] * x_coord[None] * (y_total * LZ)
        + momenta[:, 1][:, None] * y_coord * (LX * LZ)
        + momenta[:, 2][:, None] * z_coord[None] * (LX * y_total)
    )
    return jnp.mod(raw, period).astype(F32) * (TWO_PI / period)


def fused_kernel(
    norm, moms, codes, links, trig, here, above, full, both, left, rolled, right,
    part, pair, y_send, y_own, y_pair, z_send, z_land, sems, z_sems,
):
    steps, planes = part.shape[0], part.shape[2]
    rows_own = part.shape[5]
    nv, width = left.shape[1], left.shape[2]
    sites = width // 6
    half = width // 2
    rows = 16
    me = lax.axis_index("gy")
    core = lax.rem(me, 2)
    y = lax.rem(lax.div(me, 2), 2)
    z = lax.div(me, 4)
    mate = me + 1 - 2 * core
    y_mate = me + 2 - 4 * y

    def z_at(k):
        return lax.rem(z + k, planes)

    def z_peer(k):
        return 4 * z_at(k) + 2 * y + core

    barrier = pltpu.get_barrier_semaphore()
    for target in [mate, y_mate] + [z_peer(k) for k in range(1, planes)]:
        pl.semaphore_signal(barrier, inc=1, device_id={"gy": target}, device_id_type=MESH)
    pl.semaphore_wait(barrier, planes + 1)

    def remote(src, dst, pair_sems, target):
        return pltpu.make_async_remote_copy(
            src_ref=src,
            dst_ref=dst,
            send_sem=pair_sems[0],
            recv_sem=pair_sems[1],
            device_id={"gy": target},
            device_id_type=MESH,
        )

    def flat(kind, u):
        return sems.at[2 * kind, u], sems.at[2 * kind + 1, u]

    def along(kind, u, k):
        return z_sems.at[2 * kind, u, k], z_sems.at[2 * kind + 1, u, k]

    def core_copy(u):
        return remote(part.at[u, :, :, :, 1 - core], pair.at[u], flat(0, u), mate)

    def y_copy(u):
        return remote(y_send.at[u], y_pair.at[u], flat(1, u), y_mate)

    def z_copy(u, k):
        return remote(z_send.at[u, :, z_at(k)], z_land.at[u, k], along(0, u, k), z_peer(k))

    def z_gather(u, k):
        ref = full.at[u, :, z, y, core]
        return remote(ref, ref, along(1, u, k), z_peer(k))

    def y_gather(u):
        ref = full.at[u, :, :, y, core]
        return remote(ref, ref, flat(2, u), y_mate)

    def core_gather(u):
        ref = full.at[u, :, :, :, core]
        return remote(ref, ref, flat(3, u), mate)

    both[0] = here[...]
    both[1] = above[...]

    def prepare(d):
        forward_y = codes[d, 0] == 1
        forward_z = codes[d, 1] == 1
        src = jnp.where(forward_y, 1, 0)

        @pl.loop(0, nv // rows)
        def _(k):
            at = pl.ds(pl.multiple_of(k * rows, rows), rows)
            whole = both[1 - src, at, :]
            left[0, at, :] = whole
            left[1, at, :] = jnp.concatenate([-whole[:, half:], whole[:, :half]], axis=1)
            for c in range(6):
                piece = both[src, at, c * sites : (c + 1) * sites].astype(F32)
                rolled[at, c * sites : (c + 1) * sites] = jnp.where(
                    forward_z, pltpu.roll(piece, sites - LX, 1), pltpu.roll(piece, LX, 1)
                )

        for lt in range(sites // 128):
            lanes = slice(lt * 128, (lt + 1) * 128)
            m = [jnp.broadcast_to(links[d, q : q + 1, lanes], (8, 128)) for q in range(18)]
            tr = [jnp.broadcast_to(trig[d, q : q + 1, lanes], (8, 128)) for q in range(2 * moms)]

            @pl.loop(0, nv // rows)
            def _(k):
                at = pl.ds(pl.multiple_of(k * rows, rows), rows)
                halves = []
                for h in range(2):
                    sub = pl.ds(pl.multiple_of(k * rows + 8 * h, 8), 8)
                    v = [
                        rolled[sub, c * sites + lt * 128 : c * sites + (lt + 1) * 128]
                        for c in range(6)
                    ]
                    us = []
                    for r in range(3):
                        re = m[3 * r] * v[0] - m[9 + 3 * r] * v[3]
                        im = m[3 * r] * v[3] + m[9 + 3 * r] * v[0]
                        for c in range(1, 3):
                            re = re + m[3 * r + c] * v[c] - m[9 + 3 * r + c] * v[3 + c]
                            im = im + m[3 * r + c] * v[3 + c] + m[9 + 3 * r + c] * v[c]
                        us.append((re, im))
                    halves.append(us)
                for p in range(moms):
                    for r in range(3):
                        res, ims = [], []
                        for h in range(2):
                            re, im = halves[h][r]
                            res.append(tr[p] * re + tr[moms + p] * im)
                            ims.append(tr[p] * im - tr[moms + p] * re)
                        off = r * sites + lt * 128
                        right[p, at, off : off + 128] = jnp.concatenate(res, axis=0).astype(BF)
                        off = off + half
                        right[p, at, off : off + 128] = jnp.concatenate(ims, axis=0).astype(BF)

    def product(t):
        p = lax.rem(t, moms)
        for c in range(2):
            block = lax.dot_general(
                left[c], right[p], (((1,), (1,)), ((), ())), preferred_element_type=F32
            )
            part[t, c] = block.reshape(planes, 2, 2, rows_own, nv).astype(BF)
        core_copy(t).start()

    def join_cores(u):
        core_copy(u).wait_recv()
        away = part[u, :, :, 1 - y, core].astype(F32) + pair[u, :, :, 1 - y].astype(F32)
        y_send[u] = away.astype(BF)
        y_copy(u).start()
        y_own[u] = part[u, :, :, y, core].astype(F32) + pair[u, :, :, y].astype(F32)

    def join_y(u):
        y_copy(u).wait_recv()
        total = y_own[u] + y_pair[u].astype(F32)
        y_own[u] = total
        z_send[u] = total.astype(BF)
        for k in range(1, planes):
            z_copy(u, k).start()

    def join_z(u):
        for k in range(1, planes):
            z_copy(u, k).wait_recv()
        total = y_own[u, :, z]
        for k in range(1, planes):
            total = total + z_land[u, k].astype(F32)
        full[u, :, z, y, core] = (total * norm).astype(BF)
        for k in range(1, planes):
            z_gather(u, k).start()

    def share_y(u):
        for k in range(1, planes):
            z_gather(u, k).wait_recv()
        y_gather(u).start()

    def share_core(u):
        y_gather(u).wait_recv()
        core_gather(u).start()

    def finish(u):
        core_gather(u).wait()
        core_copy(u).wait_send()
        y_copy(u).wait_send()
        y_gather(u).wait_send()
        for k in range(1, planes):
            z_copy(u, k).wait_send()
            z_gather(u, k).wait_send()

    stages = [product, join_cores, join_y, join_z, share_y, share_core, finish]

    @pl.loop(0, steps + len(stages) - 1)
    def _(t):
        @pl.when(jnp.logical_and(t < steps, lax.rem(t, moms) == 0))
        def _():
            prepare(lax.div(t, moms))

        for lag, stage in enumerate(stages):
            @pl.when(jnp.logical_and(t >= lag, t - lag < steps))
            def _():
                stage(t - lag)


def contract_kernel(left, right, out):
    nv = out.shape[5]
    for d in range(out.shape[2]):
        for p in range(out.shape[3]):
            block = jnp.dot(
                left[0], right[d * out.shape[3] + p], preferred_element_type=F32
            )
            out[0, :, d, p] = block.reshape(-1, 2, nv).astype(BF)


def shards(vectors, gauge_links, perambulators, momenta, path_codes, source_times):
    nv = vectors.shape[0]
    sites = vectors.shape[4]
    size = lax.axis_size("gy")
    y_total = vectors.shape[3] * size
    moms = momenta.shape[0]
    paths = path_codes.shape[0]
    down = [((i + 1) % size, i) for i in range(size)]
    lead = jnp.transpose(vectors, (0, 2, 3, 1, 4))
    lead_up = lax.ppermute(lead, "gy", down)
    links_up = lax.ppermute(gauge_links[1], "gy", down)
    here = jnp.transpose(lead, (0, 3, 1, 2, 4)).reshape(nv, 6 * sites)
    above = jnp.transpose(lead_up, (0, 3, 1, 2, 4)).reshape(nv, 6 * sites)

    link_y = gauge_links[0, :, :, :, 0].astype(F32)
    link_z = gauge_links[1, :, :, :, 0].astype(F32)
    link_z_up = links_up[:, :, :, 0].astype(F32)
    y_here = lax.axis_index("gy")
    links, trig = [], []
    for d in range(paths):
        links.append(path_link(link_y, link_z, link_z_up, path_codes[d]))
        angles = phase_angles(momenta, y_here + jnp.where(path_codes[d, 0] == 1, 0, 1), y_total)
        trig.append(jnp.concatenate([jnp.cos(angles), jnp.sin(angles)]))
    links = jnp.stack(links).reshape(paths, 18, sites)
    trig = jnp.stack(trig)

    rows = nv // size
    steps, planes = paths * moms, size // 4
    norm = 1.0 / math.sqrt(6 * y_total * sites)
    vmem = pl.BlockSpec(memory_space=pltpu.VMEM)
    right = pl.pallas_call(
        functools.partial(fused_kernel, norm, moms),
        out_shape=jax.ShapeDtypeStruct((steps, 2, planes, 2, 2, rows, nv), BF),
        in_specs=[pl.BlockSpec(memory_space=pltpu.SMEM), vmem, vmem, vmem, vmem],
        out_specs=vmem,
        scratch_shapes=[
            pltpu.VMEM((2, nv, 6 * sites), BF),
            pltpu.VMEM((2, nv, 6 * sites), BF),
            pltpu.VMEM((nv, 6 * sites), F32),
            pltpu.VMEM((moms, nv, 6 * sites), BF),
            pltpu.VMEM((steps, 2, planes, 2, 2, rows, nv), BF),
            pltpu.VMEM((steps, 2, planes, 2, rows, nv), BF),
            pltpu.VMEM((steps, 2, planes, rows, nv), BF),
            pltpu.VMEM((steps, 2, planes, rows, nv), F32),
            pltpu.VMEM((steps, 2, planes, rows, nv), BF),
            pltpu.VMEM((steps, 2, planes, rows, nv), BF),
            pltpu.VMEM((steps, planes, 2, rows, nv), BF),
            pltpu.SemaphoreType.DMA((8, steps)),
            pltpu.SemaphoreType.DMA((4, steps, planes)),
        ],
        compiler_params=pltpu.CompilerParams(
            collective_id=0, has_side_effects=True, vmem_limit_bytes=60 * 2**20
        ),
    )(path_codes, links, trig, here, above).reshape(steps, 2 * nv, nv)

    chosen = perambulators[source_times]
    times, spins, sources = chosen.shape[:3]
    own = chosen.shape[4]
    re, im = chosen[:, :, :, 0], chosen[:, :, :, 1]
    left = jnp.stack(
        [jnp.concatenate([re, -im], axis=-1), jnp.concatenate([im, re], axis=-1)], axis=4
    ).reshape(times, spins * sources * own * 2, 2 * nv)
    count = spins * sources * own
    out = pl.pallas_call(
        contract_kernel,
        grid=(times,),
        out_shape=jax.ShapeDtypeStruct((times, count, paths, moms, 2, nv), BF),
        in_specs=[
            pl.BlockSpec((1, 2 * count, 2 * nv), lambda s: (s, 0, 0)),
            pl.BlockSpec((steps, 2 * nv, nv), lambda s: (0, 0, 0)),
        ],
        out_specs=pl.BlockSpec((1, count, paths, moms, 2, nv), lambda s: (s, 0, 0, 0, 0, 0)),
        compiler_params=pltpu.CompilerParams(vmem_limit_bytes=60 * 2**20),
    )(left, right)
    return out.reshape(times, spins, sources, own, paths, moms, 2, nv)


def solution(mesh):
    placed = (
        P("grp", None, None, "gy", None),
        P("grp", None, None, None, "gy", None),
        P("grp", None, None, None, "gy", None),
        P(),
        P(),
        P("grp"),
    )
    return jax.shard_map(
        shards,
        mesh=mesh,
        in_specs=placed,
        out_specs=P("grp", None, None, "gy", None, None, None, None),
        check_vma=False,
    )
```

time: 119 us -> 98.6 us (0.83)
  the two profiles are of different devices: /device:TPU:31 before, /device:TPU:0 now
where the time goes in v2:
time: 98.6 us; the launch traced here: 98.1 us
  Pallas kernels  64.7 us (66%)
  local copies, waits for them, and re-layouts  16.7 us (17%)
  starting transfers between devices  6.15 us (6%)
  other arithmetic  4.85 us (5%)
  between operations  2.98 us (3%)
  waiting for transfers between devices  2.68 us (3%)
    pallas_call x1, Pallas kernels, shards(): pl.pallas_call(functools.partial(fused_kernel, norm, moms), out_shape=jax...  57.7 us
    pallas_call x1, Pallas kernels, shards(): pl.pallas_call(contract_kernel, grid=(times,), out_shape=jax.ShapeDtypeSt...  7.01 us
    ppermute x1, starting transfers between devices, shards(): links_up = lax.ppermute(gauge_links[1], 'gy', down)  5.47 us
    unnamed x33, local copies, waits for them, and re-layouts  5.39 us
    ppermute x1, waiting for transfers between devices, shards(): lead_up = lax.ppermute(lead, 'gy', down)  2.67 us
    reshape x1, local copies, waits for them, and re-layouts, shards(): here = jnp.transpose(lead, (0, 3, 1, 2, 4)).reshape(nv, 6 * sites)  2.58 us
    reshape x1, local copies, waits for them, and re-layouts, shards(): above = jnp.transpose(lead_up, (0, 3, 1, 2, 4)).reshape(nv, 6 * sites)  2.58 us
  transfers between devices with their start and end apart: 2, of which 1 were waited for; matrix products, arithmetic and copies ran while one was open for 17% of the time, Pallas kernels for 0%

profile of v2, /device:TPU:0, one launch (start us, length us, event | category | flops | bytes accessed | tf_op | source)
XLA Modules:
  0.0 98.1 jit_solution(6177163299582559000)
XLA Ops:
  0.0 0.0 copy-start
  0.0 1.5 %slice_bitcast_fusion.2 = bf16[2,3,3,1,512]{4,0,2,1,3:T(2,128)(2,1)} fusion(bf16[2,2,3,3,1,512]{5,1,3,2,4,0:T(2,128)(2,1)} %bitcast.109), kind=kLoop, calls=%fused_computation.94 | loop fusion | bytes 36864 | tf_op jit(solution)/shard_map/squeeze | solution.py:259
  1.5 0.0 copy-start.1
  1.5 0.0 copy-start.7
  1.5 0.0 copy-start.10
  1.5 5.5 %collective-permute-start = (bf16[2,3,3,1,512]{4,0,2,1,3:T(2,128)(2,1)}, bf16[2,3,3,1,512]{4,0,2,1,3:T(2,128)(2,1)}, u32[]{:S(2)}, u32[]{:S(2)}) collective-permute-start(bf16[2,3,3,1,512]{4,0,2,1,3:T(2,128)(2,1)} %slice_bitcast_fusion.2), channel_id=1, source_target_pairs={{1,0},{2,1},{3,2},{4,3},{5,4},{6,5},{7,6},{8,7},{9,8},{10,9},{11,1... | collective-permute-start | bytes 55304 | tf_op jit(solution)/shard_map/ppermute | solution.py:259
  7.0 4.9 %copy.41 = bf16[256,2,3,1,512]{0,4,2,1,3:T(8,128)(2,1)} copy(bf16[256,2,3,1,512]{4,1,3,2,0:T(2,128)(2,1)} %param.6) | data formatting | bytes 3145728 | tf_op args[0]
  11.8 0.7 collective-permute-start.1
  12.5 0.6 add_select_fusion.3
  13.1 0.6 add_select_fusion.2
  13.7 0.0 copy-done.1
  13.7 0.0 copy-done.7
  13.7 0.7 fusion.25
  15.7 0.1 broadcast_select_fusion.1
  15.8 0.1 slice.190
  15.9 0.1 slice.200
  16.0 0.7 fusion.19
  16.7 0.0 copy-done.10
  16.7 0.0 copy-done
  16.7 0.6 gather_fusion
  17.3 0.1 slice_bitcast_fusion
  17.4 0.1 fusion.1
  17.5 0.1 fusion
  17.6 0.0 copy-start.6
  17.7 0.0 copy-start.8
  17.7 0.0 copy-start.9
  17.7 0.1 maximum_bitcast_fusion
  17.8 0.0 copy-start.5
  17.8 0.0 copy-start.4
  17.8 0.0 copy-start.3
  17.8 0.0 copy-start.2
  17.8 0.1 pad_maximum_fusion
  17.9 0.4 copy-done.6
  18.3 0.2 multiply_reduce_fusion.1
  18.5 0.0 copy-done.8
  18.5 0.0 copy-done.9
  18.6 0.2 fusion.11
  18.8 0.6 pad_maximum_fusion.7.trig
  20.6 0.0 copy-done.5
  20.6 0.0 copy-done.4
  20.7 0.0 copy-done.3
  20.7 0.0 copy-done.2
  20.7 1.1 %copy.32 = bf16[4,4,2,16,2,512]{5,4,3,2,1,0:T(2,128)(2,1)S(1)} copy(bf16[4,4,2,16,2,512]{5,3,2,1,0,4:T(8,128)(2,1)S(1)} %pad_maximum_fusion) | data formatting | bytes 2097152 | tf_op jit(solution)/shard_map/stack | solution.py:308
  21.8 1.2 %reshape.168.left = bf16[4,256,512]{2,1,0:T(8,128)(2,1)} reshape(bf16[4,4,2,16,2,512]{5,4,3,2,1,0:T(2,128)(2,1)S(1)} %copy.32) | data formatting | bytes 2097152 | tf_op jit(solution)/shard_map/reshape | solution.py:310
  23.0 2.6 %copy.43.here = bf16[256,3072]{1,0:T(8,128)(2,1)} copy(bf16[256,3072]{0,1:T(8,128)(2,1)} %bitcast.98) | data formatting | bytes 3145728 | tf_op jit(solution)/shard_map/reshape | solution.py:260
  25.6 0.0 collective-permute-done
  25.6 0.8 convert_select_fusion.1
  26.4 0.1 subtract_reduce_fusion
  26.5 0.1 pad_maximum_fusion.10
  26.7 0.1 subtract_reduce_fusion.2
  26.8 0.1 pad_maximum_fusion.11
  26.9 0.1 fusion.20
  27.0 0.1 subtract_reduce_fusion.3
  27.1 0.1 subtract_reduce_fusion.1
  27.3 0.1 maximum_select_fusion
  27.3 0.1 maximum_select_fusion.1
  27.4 0.7 pad_maximum_fusion.1.links
  28.1 2.7 %collective-permute-done.1 = bf16[256,3,1,2,512]{0,4,1,3,2:T(8,128)(2,1)} collective-permute-done((bf16[256,3,1,2,512]{0,4,1,3,2:T(8,128)(2,1)}, bf16[256,3,1,2,512]{0,4,1,3,2:T(8,128)(2,1)}, u32[]{:S(2)}, u32[]{:S(2)}) %collective-permute-start.1) | collective-permute-done | bytes 1572896 | tf_op jit(solution)/shard_map/ppermute | solution.py:258
  30.8 2.6 %copy.44.above = bf16[256,3072]{1,0:T(8,128)(2,1)} copy(bf16[256,3072]{0,1:T(8,128)(2,1)} %bitcast.36) | data formatting | bytes 3145728 | tf_op jit(solution)/shard_map/reshape | solution.py:261
  33.3 57.7 %shard_map.64 = bf16[8,2,4,2,2,16,256]{6,5,4,3,2,1,0:T(8,128)(2,1)} custom-call(s32[2,2]{1,0:T(2,128)} %codes.1, f32[2,18,512]{2,1,0:T(8,128)} %pad_maximum_fusion.1.links, f32[2,8,512]{2,1,0:T(8,128)} %pad_maximum_fusion.7.trig, bf16[256,3072]{1,0:T(8,128)(2,1)} %copy.43.here, bf16[256,3072]{1,0:T(8,128)(2,1)} %copy.44.above), custom_call_target="tpu_custom_call" | custom-call | tf_op jit(solution)/shard_map/pallas_call | solution.py:279
  91.1 7.0 %shard_map.65 = bf16[4,128,2,4,2,256]{5,4,3,2,1,0:T(2,128)(2,1)} custom-call(bf16[4,256,512]{2,1,0:T(8,128)(2,1)} %reshape.168.left, bf16[8,512,256]{2,1,0:T(8,128)(2,1)} %bitcast.96), custom_call_target="tpu_custom_call" | custom-call | tf_op jit(solution)/shard_map/pallas_call | solution.py:312
  (32 shorter events, 0.5 us)
Async XLA Ops:
  0.0 16.7 %copy-start = (bf16[16,4,2,2,16,256]{5,4,3,2,1,0:T(8,128)(2,1)S(1)}, bf16[16,4,2,2,16,256]{5,4,3,2,1,0:T(8,128)(2,1)}, u32[]{:S(2)}) copy-start(bf16[16,4,2,2,16,256]{5,4,3,2,1,0:T(8,128)(2,1)} %param.8) | copy-start | bytes 6291460
  1.5 12.2 %copy-start.1 = (bf16[2,2,3,3,1,512]{5,1,4,3,2,0:T(2,128)(2,1)S(1)}, bf16[2,2,3,3,1,512]{5,1,4,3,2,0:T(2,128)(2,1)}, u32[]{:S(2)}) copy-start(bf16[2,2,3,3,1,512]{5,1,4,3,2,0:T(2,128)(2,1)} %param.7) | copy-start | bytes 110596
  1.5 12.2 %copy-start.7 = (s32[2,2]{1,0:T(2,128)S(1)}, s32[2,2]{1,0:T(2,128)}, u32[]{:S(2)}) copy-start(s32[2,2]{1,0:T(2,128)} %codes.1) | copy-start | bytes 52
  1.5 15.2 %copy-start.10 = (s32[4]{0:T(128)S(1)}, s32[4]{0:T(128)}, u32[]{:S(2)}) copy-start(s32[4]{0:T(128)} %param.11) | copy-start | bytes 52
  1.5 24.1 %collective-permute-start = (bf16[2,3,3,1,512]{4,0,2,1,3:T(2,128)(2,1)}, bf16[2,3,3,1,512]{4,0,2,1,3:T(2,128)(2,1)}, u32[]{:S(2)}, u32[]{:S(2)}) collective-permute-start(bf16[2,3,3,1,512]{4,0,2,1,3:T(2,128)(2,1)} %slice_bitcast_fusion.2), channel_id=1, source_target_pairs={{1,0},{2,1},{3,2},{4,3},{5,4},{6,5},{7,6},{8,7},{9,8},{10,9},{11,1... | collective-permute-start | bytes 55304 | tf_op jit(solution)/shard_map/ppermute | solution.py:259
  11.8 18.9 %collective-permute-start.1 = (bf16[256,3,1,2,512]{0,4,1,3,2:T(8,128)(2,1)}, bf16[256,3,1,2,512]{0,4,1,3,2:T(8,128)(2,1)}, u32[]{:S(2)}, u32[]{:S(2)}) collective-permute-start(bf16[256,3,1,2,512]{0,4,1,3,2:T(8,128)(2,1)} %bitcast.97), channel_id=1, source_target_pairs={{1,0},{2,1},{3,2},{4,3},{5,4},{6,5},{7,6},{8,7},{9,8},{10,9},{11,1... | collective-permute-start | bytes 4718600 | tf_op jit(solution)/shard_map/ppermute | solution.py:258
  17.6 0.7 copy-start.6
  17.7 0.9 copy-start.8
  17.7 0.9 copy-start.9
  17.8 2.8 %copy-start.5 = (f32[1,3,3,512]{3,0,2,1:T(1,128)S(1)}, f32[1,3,3,512]{3,0,2,1:T(1,128)}, u32[]{:S(2)}) copy-start(f32[1,3,3,512]{3,0,2,1:T(1,128)} %get-tuple-element.31) | copy-start | bytes 55300
  17.8 2.8 %copy-start.4 = (f32[1,3,3,512]{3,0,2,1:T(1,128)S(1)}, f32[1,3,3,512]{3,0,2,1:T(1,128)}, u32[]{:S(2)}) copy-start(f32[1,3,3,512]{3,0,2,1:T(1,128)} %get-tuple-element.32) | copy-start | bytes 55300
  17.8 2.8 %copy-start.3 = (f32[1,3,3,512]{3,0,2,1:T(1,128)S(1)}, f32[1,3,3,512]{3,0,2,1:T(1,128)}, u32[]{:S(2)}) copy-start(f32[1,3,3,512]{3,0,2,1:T(1,128)} %get-tuple-element.53) | copy-start | bytes 55300
  17.8 2.9 %copy-start.2 = (f32[1,3,3,512]{3,0,2,1:T(1,128)S(1)}, f32[1,3,3,512]{3,0,2,1:T(1,128)}, u32[]{:S(2)}) copy-start(f32[1,3,3,512]{3,0,2,1:T(1,128)} %get-tuple-element.54) | copy-start | bytes 55300

commit v3 on v2

--- a/solution.py
+++ b/solution.py
@@ -222,18 +222,22 @@
             z_copy(u, k).wait_send()
             z_gather(u, k).wait_send()
 
-    stages = [product, join_cores, join_y, join_z, share_y, share_core, finish]
-
-    @pl.loop(0, steps + len(stages) - 1)
+    stages = [
+        (product, 0), (join_cores, 1), (join_y, 3), (join_z, 5),
+        (share_y, 7), (share_core, 9), (finish, 10),
+    ]
+    prepare(0)
+
+    @pl.loop(0, steps + stages[-1][1])
     def _(t):
-        @pl.when(jnp.logical_and(t < steps, lax.rem(t, moms) == 0))
-        def _():
-            prepare(lax.div(t, moms))
-
-        for lag, stage in enumerate(stages):
+        for stage, lag in stages:
             @pl.when(jnp.logical_and(t >= lag, t - lag < steps))
             def _():
                 stage(t - lag)
+
+        @pl.when(jnp.logical_and(t < steps - 1, lax.rem(t + 1, moms) == 0))
+        def _():
+            prepare(lax.div(t + 1, moms))
 
 
 def contract_kernel(left, right, out):

time: 98.6 us -> 95.5 us (0.969)
  Pallas kernels: 64.7 us -> 61.4 us
    pallas_call x1, Pallas kernels: 57.7 us -> 54.4 us  [shards(): pl.pallas_call(functools.partial(fused_kernel, norm, moms), out_shape=jax...]
  transfers between devices with their start and end apart: 2 -> 2, of which waited for: 1 -> 1; matrix products, arithmetic and copies ran while one was open for 17% -> 18% of each run, Pallas kernels for 0% -> 0%
where the time goes in v3:
time: 95.5 us; the launch traced here: 94.8 us
  Pallas kernels  61.4 us (64%)
  local copies, waits for them, and re-layouts  16.7 us (17%)
  starting transfers between devices  6.15 us (6%)
  other arithmetic  4.85 us (5%)
  between operations  2.98 us (3%)
  waiting for transfers between devices  2.68 us (3%)
    pallas_call x1, Pallas kernels, shards(): pl.pallas_call(functools.partial(fused_kernel, norm, moms), out_shape=jax...  54.4 us
    pallas_call x1, Pallas kernels, shards(): pl.pallas_call(contract_kernel, grid=(times,), out_shape=jax.ShapeDtypeSt...  7 us
    ppermute x1, starting transfers between devices, shards(): links_up = lax.ppermute(gauge_links[1], 'gy', down)  5.47 us
    unnamed x33, local copies, waits for them, and re-layouts  5.39 us
    ppermute x1, waiting for transfers between devices, shards(): lead_up = lax.ppermute(lead, 'gy', down)  2.67 us
    reshape x1, local copies, waits for them, and re-layouts, shards(): here = jnp.transpose(lead, (0, 3, 1, 2, 4)).reshape(nv, 6 * sites)  2.58 us
    reshape x1, local copies, waits for them, and re-layouts, shards(): above = jnp.transpose(lead_up, (0, 3, 1, 2, 4)).reshape(nv, 6 * sites)  2.58 us
  transfers between devices with their start and end apart: 2, of which 1 were waited for; matrix products, arithmetic and copies ran while one was open for 18% of the time, Pallas kernels for 0%

profile of v3, /device:TPU:0, one launch (start us, length us, event | category | flops | bytes accessed | tf_op | source)
XLA Modules:
  0.0 94.8 jit_solution(16850256639054290623)
XLA Ops:
  0.0 0.0 copy-start
  0.0 1.5 %slice_bitcast_fusion.2 = bf16[2,3,3,1,512]{4,0,2,1,3:T(2,128)(2,1)} fusion(bf16[2,2,3,3,1,512]{5,1,3,2,4,0:T(2,128)(2,1)} %bitcast.109), kind=kLoop, calls=%fused_computation.94 | loop fusion | bytes 36864 | tf_op jit(solution)/shard_map/squeeze | solution.py:263
  1.5 0.0 copy-start.1
  1.5 0.0 copy-start.7
  1.5 0.0 copy-start.10
  1.5 5.5 %collective-permute-start = (bf16[2,3,3,1,512]{4,0,2,1,3:T(2,128)(2,1)}, bf16[2,3,3,1,512]{4,0,2,1,3:T(2,128)(2,1)}, u32[]{:S(2)}, u32[]{:S(2)}) collective-permute-start(bf16[2,3,3,1,512]{4,0,2,1,3:T(2,128)(2,1)} %slice_bitcast_fusion.2), channel_id=1, source_target_pairs={{1,0},{2,1},{3,2},{4,3},{5,4},{6,5},{7,6},{8,7},{9,8},{10,9},{11,1... | collective-permute-start | bytes 55304 | tf_op jit(solution)/shard_map/ppermute | solution.py:263
  7.0 4.9 %copy.41 = bf16[256,2,3,1,512]{0,4,2,1,3:T(8,128)(2,1)} copy(bf16[256,2,3,1,512]{4,1,3,2,0:T(2,128)(2,1)} %param.6) | data formatting | bytes 3145728 | tf_op args[0]
  11.8 0.7 collective-permute-start.1
  12.5 0.6 add_select_fusion.3
  13.1 0.6 add_select_fusion.2
  13.7 0.0 copy-done.1
  13.7 0.0 copy-done.7
  13.7 0.7 fusion.25
  15.7 0.1 broadcast_select_fusion.1
  15.8 0.1 slice.190
  15.9 0.1 slice.200
  16.0 0.7 fusion.19
  16.7 0.0 copy-done.10
  16.7 0.0 copy-done
  16.7 0.6 gather_fusion
  17.3 0.1 slice_bitcast_fusion
  17.4 0.1 fusion.1
  17.5 0.1 fusion
  17.6 0.0 copy-start.6
  17.7 0.0 copy-start.8
  17.7 0.0 copy-start.9
  17.7 0.1 maximum_bitcast_fusion
  17.8 0.0 copy-start.5
  17.8 0.0 copy-start.4
  17.8 0.0 copy-start.3
  17.8 0.0 copy-start.2
  17.8 0.1 pad_maximum_fusion
  17.9 0.4 copy-done.6
  18.3 0.2 multiply_reduce_fusion.1
  18.5 0.0 copy-done.8
  18.5 0.0 copy-done.9
  18.6 0.2 fusion.11
  18.8 0.6 pad_maximum_fusion.7.trig
  20.6 0.0 copy-done.5
  20.6 0.0 copy-done.4
  20.7 0.0 copy-done.3
  20.7 0.0 copy-done.2
  20.7 1.1 %copy.32 = bf16[4,4,2,16,2,512]{5,4,3,2,1,0:T(2,128)(2,1)S(1)} copy(bf16[4,4,2,16,2,512]{5,3,2,1,0,4:T(8,128)(2,1)S(1)} %pad_maximum_fusion) | data formatting | bytes 2097152 | tf_op jit(solution)/shard_map/stack | solution.py:312
  21.8 1.2 %reshape.168.left = bf16[4,256,512]{2,1,0:T(8,128)(2,1)} reshape(bf16[4,4,2,16,2,512]{5,4,3,2,1,0:T(2,128)(2,1)S(1)} %copy.32) | data formatting | bytes 2097152 | tf_op jit(solution)/shard_map/reshape | solution.py:314
  23.0 2.6 %copy.43.here = bf16[256,3072]{1,0:T(8,128)(2,1)} copy(bf16[256,3072]{0,1:T(8,128)(2,1)} %bitcast.98) | data formatting | bytes 3145728 | tf_op jit(solution)/shard_map/reshape | solution.py:264
  25.6 0.0 collective-permute-done
  25.6 0.8 convert_select_fusion.1
  26.4 0.1 subtract_reduce_fusion
  26.5 0.1 pad_maximum_fusion.10
  26.7 0.1 subtract_reduce_fusion.2
  26.8 0.1 pad_maximum_fusion.11
  26.9 0.1 fusion.20
  27.0 0.1 subtract_reduce_fusion.3
  27.1 0.1 subtract_reduce_fusion.1
  27.3 0.1 maximum_select_fusion
  27.3 0.1 maximum_select_fusion.1
  27.4 0.7 pad_maximum_fusion.1.links
  28.1 2.7 %collective-permute-done.1 = bf16[256,3,1,2,512]{0,4,1,3,2:T(8,128)(2,1)} collective-permute-done((bf16[256,3,1,2,512]{0,4,1,3,2:T(8,128)(2,1)}, bf16[256,3,1,2,512]{0,4,1,3,2:T(8,128)(2,1)}, u32[]{:S(2)}, u32[]{:S(2)}) %collective-permute-start.1) | collective-permute-done | bytes 1572896 | tf_op jit(solution)/shard_map/ppermute | solution.py:262
  30.8 2.6 %copy.44.above = bf16[256,3072]{1,0:T(8,128)(2,1)} copy(bf16[256,3072]{0,1:T(8,128)(2,1)} %bitcast.36) | data formatting | bytes 3145728 | tf_op jit(solution)/shard_map/reshape | solution.py:265
  33.3 54.4 %shard_map.64 = bf16[8,2,4,2,2,16,256]{6,5,4,3,2,1,0:T(8,128)(2,1)} custom-call(s32[2,2]{1,0:T(2,128)} %codes.1, f32[2,18,512]{2,1,0:T(8,128)} %pad_maximum_fusion.1.links, f32[2,8,512]{2,1,0:T(8,128)} %pad_maximum_fusion.7.trig, bf16[256,3072]{1,0:T(8,128)(2,1)} %copy.43.here, bf16[256,3072]{1,0:T(8,128)(2,1)} %copy.44.above), custom_call_target="tpu_custom_call" | custom-call | tf_op jit(solution)/shard_map/pallas_call | solution.py:283
  87.8 7.0 %shard_map.65 = bf16[4,128,2,4,2,256]{5,4,3,2,1,0:T(2,128)(2,1)} custom-call(bf16[4,256,512]{2,1,0:T(8,128)(2,1)} %reshape.168.left, bf16[8,512,256]{2,1,0:T(8,128)(2,1)} %bitcast.96), custom_call_target="tpu_custom_call" | custom-call | tf_op jit(solution)/shard_map/pallas_call | solution.py:316
  (32 shorter events, 0.5 us)
Async XLA Ops:
  0.0 16.7 %copy-start = (bf16[16,4,2,2,16,256]{5,4,3,2,1,0:T(8,128)(2,1)S(1)}, bf16[16,4,2,2,16,256]{5,4,3,2,1,0:T(8,128)(2,1)}, u32[]{:S(2)}) copy-start(bf16[16,4,2,2,16,256]{5,4,3,2,1,0:T(8,128)(2,1)} %param.8) | copy-start | bytes 6291460
  1.5 12.2 %copy-start.1 = (bf16[2,2,3,3,1,512]{5,1,4,3,2,0:T(2,128)(2,1)S(1)}, bf16[2,2,3,3,1,512]{5,1,4,3,2,0:T(2,128)(2,1)}, u32[]{:S(2)}) copy-start(bf16[2,2,3,3,1,512]{5,1,4,3,2,0:T(2,128)(2,1)} %param.7) | copy-start | bytes 110596
  1.5 12.2 %copy-start.7 = (s32[2,2]{1,0:T(2,128)S(1)}, s32[2,2]{1,0:T(2,128)}, u32[]{:S(2)}) copy-start(s32[2,2]{1,0:T(2,128)} %codes.1) | copy-start | bytes 52
  1.5 15.2 %copy-start.10 = (s32[4]{0:T(128)S(1)}, s32[4]{0:T(128)}, u32[]{:S(2)}) copy-start(s32[4]{0:T(128)} %param.11) | copy-start | bytes 52
  1.5 24.1 %collective-permute-start = (bf16[2,3,3,1,512]{4,0,2,1,3:T(2,128)(2,1)}, bf16[2,3,3,1,512]{4,0,2,1,3:T(2,128)(2,1)}, u32[]{:S(2)}, u32[]{:S(2)}) collective-permute-start(bf16[2,3,3,1,512]{4,0,2,1,3:T(2,128)(2,1)} %slice_bitcast_fusion.2), channel_id=1, source_target_pairs={{1,0},{2,1},{3,2},{4,3},{5,4},{6,5},{7,6},{8,7},{9,8},{10,9},{11,1... | collective-permute-start | bytes 55304 | tf_op jit(solution)/shard_map/ppermute | solution.py:263
  11.8 18.9 %collective-permute-start.1 = (bf16[256,3,1,2,512]{0,4,1,3,2:T(8,128)(2,1)}, bf16[256,3,1,2,512]{0,4,1,3,2:T(8,128)(2,1)}, u32[]{:S(2)}, u32[]{:S(2)}) collective-permute-start(bf16[256,3,1,2,512]{0,4,1,3,2:T(8,128)(2,1)} %bitcast.97), channel_id=1, source_target_pairs={{1,0},{2,1},{3,2},{4,3},{5,4},{6,5},{7,6},{8,7},{9,8},{10,9},{11,1... | collective-permute-start | bytes 4718600 | tf_op jit(solution)/shard_map/ppermute | solution.py:262
  17.6 0.7 copy-start.6
  17.7 0.9 copy-start.8
  17.7 0.9 copy-start.9
  17.8 2.8 %copy-start.5 = (f32[1,3,3,512]{3,0,2,1:T(1,128)S(1)}, f32[1,3,3,512]{3,0,2,1:T(1,128)}, u32[]{:S(2)}) copy-start(f32[1,3,3,512]{3,0,2,1:T(1,128)} %get-tuple-element.31) | copy-start | bytes 55300
  17.8 2.8 %copy-start.4 = (f32[1,3,3,512]{3,0,2,1:T(1,128)S(1)}, f32[1,3,3,512]{3,0,2,1:T(1,128)}, u32[]{:S(2)}) copy-start(f32[1,3,3,512]{3,0,2,1:T(1,128)} %get-tuple-element.32) | copy-start | bytes 55300
  17.8 2.8 %copy-start.3 = (f32[1,3,3,512]{3,0,2,1:T(1,128)S(1)}, f32[1,3,3,512]{3,0,2,1:T(1,128)}, u32[]{:S(2)}) copy-start(f32[1,3,3,512]{3,0,2,1:T(1,128)} %get-tuple-element.53) | copy-start | bytes 55300
  17.8 2.9 %copy-start.2 = (f32[1,3,3,512]{3,0,2,1:T(1,128)S(1)}, f32[1,3,3,512]{3,0,2,1:T(1,128)}, u32[]{:S(2)}) copy-start(f32[1,3,3,512]{3,0,2,1:T(1,128)} %get-tuple-element.54) | copy-start | bytes 55300

commit v4 on v3

--- a/solution.py
+++ b/solution.py
@@ -223,8 +223,8 @@
             z_gather(u, k).wait_send()
 
     stages = [
-        (product, 0), (join_cores, 1), (join_y, 3), (join_z, 5),
-        (share_y, 7), (share_core, 9), (finish, 10),
+        (product, 0), (join_cores, 1), (join_y, 4), (join_z, 7),
+        (share_y, 10), (share_core, 13), (finish, 14),
     ]
     prepare(0)
 

time: 95.5 us -> 95.4 us (level)
  no operation moved by 1% of the time
where the time goes in v4:
time: 95.4 us; the launch traced here: 94.9 us
  Pallas kernels  61.5 us (64%)
  local copies, waits for them, and re-layouts  16.7 us (18%)
  starting transfers between devices  6.15 us (6%)
  other arithmetic  4.85 us (5%)
  between operations  2.98 us (3%)
  waiting for transfers between devices  2.68 us (3%)
    pallas_call x1, Pallas kernels, shards(): pl.pallas_call(functools.partial(fused_kernel, norm, moms), out_shape=jax...  54.5 us
    pallas_call x1, Pallas kernels, shards(): pl.pallas_call(contract_kernel, grid=(times,), out_shape=jax.ShapeDtypeSt...  7 us
    ppermute x1, starting transfers between devices, shards(): links_up = lax.ppermute(gauge_links[1], 'gy', down)  5.47 us
    unnamed x33, local copies, waits for them, and re-layouts  5.39 us
    ppermute x1, waiting for transfers between devices, shards(): lead_up = lax.ppermute(lead, 'gy', down)  2.67 us
    reshape x1, local copies, waits for them, and re-layouts, shards(): here = jnp.transpose(lead, (0, 3, 1, 2, 4)).reshape(nv, 6 * sites)  2.58 us
    reshape x1, local copies, waits for them, and re-layouts, shards(): above = jnp.transpose(lead_up, (0, 3, 1, 2, 4)).reshape(nv, 6 * sites)  2.58 us
  transfers between devices with their start and end apart: 2, of which 1 were waited for; matrix products, arithmetic and copies ran while one was open for 18% of the time, Pallas kernels for 0%

profile of v4, /device:TPU:0, one launch (start us, length us, event | category | flops | bytes accessed | tf_op | source)
XLA Modules:
  0.0 94.9 jit_solution(16791479082943778055)
XLA Ops:
  0.0 0.0 copy-start
  0.0 1.5 %slice_bitcast_fusion.2 = bf16[2,3,3,1,512]{4,0,2,1,3:T(2,128)(2,1)} fusion(bf16[2,2,3,3,1,512]{5,1,3,2,4,0:T(2,128)(2,1)} %bitcast.109), kind=kLoop, calls=%fused_computation.94 | loop fusion | bytes 36864 | tf_op jit(solution)/shard_map/squeeze | solution.py:263
  1.5 0.0 copy-start.1
  1.5 0.0 copy-start.7
  1.5 0.0 copy-start.10
  1.5 5.5 %collective-permute-start = (bf16[2,3,3,1,512]{4,0,2,1,3:T(2,128)(2,1)}, bf16[2,3,3,1,512]{4,0,2,1,3:T(2,128)(2,1)}, u32[]{:S(2)}, u32[]{:S(2)}) collective-permute-start(bf16[2,3,3,1,512]{4,0,2,1,3:T(2,128)(2,1)} %slice_bitcast_fusion.2), channel_id=1, source_target_pairs={{1,0},{2,1},{3,2},{4,3},{5,4},{6,5},{7,6},{8,7},{9,8},{10,9},{11,1... | collective-permute-start | bytes 55304 | tf_op jit(solution)/shard_map/ppermute | solution.py:263
  7.0 4.9 %copy.41 = bf16[256,2,3,1,512]{0,4,2,1,3:T(8,128)(2,1)} copy(bf16[256,2,3,1,512]{4,1,3,2,0:T(2,128)(2,1)} %param.6) | data formatting | bytes 3145728 | tf_op args[0]
  11.8 0.7 collective-permute-start.1
  12.5 0.6 add_select_fusion.3
  13.1 0.6 add_select_fusion.2
  13.7 0.0 copy-done.1
  13.7 0.0 copy-done.7
  13.7 0.7 fusion.25
  15.7 0.1 broadcast_select_fusion.1
  15.8 0.1 slice.190
  15.9 0.1 slice.200
  16.0 0.7 fusion.19
  16.7 0.0 copy-done.10
  16.7 0.0 copy-done
  16.7 0.6 gather_fusion
  17.3 0.1 slice_bitcast_fusion
  17.4 0.1 fusion.1
  17.5 0.1 fusion
  17.6 0.0 copy-start.6
  17.7 0.0 copy-start.8
  17.7 0.0 copy-start.9
  17.7 0.1 maximum_bitcast_fusion
  17.8 0.0 copy-start.5
  17.8 0.0 copy-start.4
  17.8 0.0 copy-start.3
  17.8 0.0 copy-start.2
  17.8 0.1 pad_maximum_fusion
  17.9 0.4 copy-done.6
  18.3 0.2 multiply_reduce_fusion.1
  18.5 0.0 copy-done.8
  18.5 0.0 copy-done.9
  18.6 0.2 fusion.11
  18.8 0.6 pad_maximum_fusion.7.trig
  20.6 0.0 copy-done.5
  20.6 0.0 copy-done.4
  20.7 0.0 copy-done.3
  20.7 0.0 copy-done.2
  20.7 1.1 %copy.32 = bf16[4,4,2,16,2,512]{5,4,3,2,1,0:T(2,128)(2,1)S(1)} copy(bf16[4,4,2,16,2,512]{5,3,2,1,0,4:T(8,128)(2,1)S(1)} %pad_maximum_fusion) | data formatting | bytes 2097152 | tf_op jit(solution)/shard_map/stack | solution.py:312
  21.8 1.2 %reshape.168.left = bf16[4,256,512]{2,1,0:T(8,128)(2,1)} reshape(bf16[4,4,2,16,2,512]{5,4,3,2,1,0:T(2,128)(2,1)S(1)} %copy.32) | data formatting | bytes 2097152 | tf_op jit(solution)/shard_map/reshape | solution.py:314
  23.0 2.6 %copy.43.here = bf16[256,3072]{1,0:T(8,128)(2,1)} copy(bf16[256,3072]{0,1:T(8,128)(2,1)} %bitcast.98) | data formatting | bytes 3145728 | tf_op jit(solution)/shard_map/reshape | solution.py:264
  25.6 0.0 collective-permute-done
  25.6 0.8 convert_select_fusion.1
  26.4 0.1 subtract_reduce_fusion
  26.5 0.1 pad_maximum_fusion.10
  26.7 0.1 subtract_reduce_fusion.2
  26.8 0.1 pad_maximum_fusion.11
  26.9 0.1 fusion.20
  27.0 0.1 subtract_reduce_fusion.3
  27.1 0.1 subtract_reduce_fusion.1
  27.3 0.1 maximum_select_fusion
  27.3 0.1 maximum_select_fusion.1
  27.4 0.7 pad_maximum_fusion.1.links
  28.1 2.7 %collective-permute-done.1 = bf16[256,3,1,2,512]{0,4,1,3,2:T(8,128)(2,1)} collective-permute-done((bf16[256,3,1,2,512]{0,4,1,3,2:T(8,128)(2,1)}, bf16[256,3,1,2,512]{0,4,1,3,2:T(8,128)(2,1)}, u32[]{:S(2)}, u32[]{:S(2)}) %collective-permute-start.1) | collective-permute-done | bytes 1572896 | tf_op jit(solution)/shard_map/ppermute | solution.py:262
  30.8 2.6 %copy.44.above = bf16[256,3072]{1,0:T(8,128)(2,1)} copy(bf16[256,3072]{0,1:T(8,128)(2,1)} %bitcast.36) | data formatting | bytes 3145728 | tf_op jit(solution)/shard_map/reshape | solution.py:265
  33.3 54.5 %shard_map.64 = bf16[8,2,4,2,2,16,256]{6,5,4,3,2,1,0:T(8,128)(2,1)} custom-call(s32[2,2]{1,0:T(2,128)} %codes.1, f32[2,18,512]{2,1,0:T(8,128)} %pad_maximum_fusion.1.links, f32[2,8,512]{2,1,0:T(8,128)} %pad_maximum_fusion.7.trig, bf16[256,3072]{1,0:T(8,128)(2,1)} %copy.43.here, bf16[256,3072]{1,0:T(8,128)(2,1)} %copy.44.above), custom_call_target="tpu_custom_call" | custom-call | tf_op jit(solution)/shard_map/pallas_call | solution.py:283
  87.9 7.0 %shard_map.65 = bf16[4,128,2,4,2,256]{5,4,3,2,1,0:T(2,128)(2,1)} custom-call(bf16[4,256,512]{2,1,0:T(8,128)(2,1)} %reshape.168.left, bf16[8,512,256]{2,1,0:T(8,128)(2,1)} %bitcast.96), custom_call_target="tpu_custom_call" | custom-call | tf_op jit(solution)/shard_map/pallas_call | solution.py:316
  (32 shorter events, 0.5 us)
Async XLA Ops:
  0.0 16.7 %copy-start = (bf16[16,4,2,2,16,256]{5,4,3,2,1,0:T(8,128)(2,1)S(1)}, bf16[16,4,2,2,16,256]{5,4,3,2,1,0:T(8,128)(2,1)}, u32[]{:S(2)}) copy-start(bf16[16,4,2,2,16,256]{5,4,3,2,1,0:T(8,128)(2,1)} %param.8) | copy-start | bytes 6291460
  1.5 12.2 %copy-start.1 = (bf16[2,2,3,3,1,512]{5,1,4,3,2,0:T(2,128)(2,1)S(1)}, bf16[2,2,3,3,1,512]{5,1,4,3,2,0:T(2,128)(2,1)}, u32[]{:S(2)}) copy-start(bf16[2,2,3,3,1,512]{5,1,4,3,2,0:T(2,128)(2,1)} %param.7) | copy-start | bytes 110596
  1.5 12.2 %copy-start.7 = (s32[2,2]{1,0:T(2,128)S(1)}, s32[2,2]{1,0:T(2,128)}, u32[]{:S(2)}) copy-start(s32[2,2]{1,0:T(2,128)} %codes.1) | copy-start | bytes 52
  1.5 15.2 %copy-start.10 = (s32[4]{0:T(128)S(1)}, s32[4]{0:T(128)}, u32[]{:S(2)}) copy-start(s32[4]{0:T(128)} %param.11) | copy-start | bytes 52
  1.5 24.1 %collective-permute-start = (bf16[2,3,3,1,512]{4,0,2,1,3:T(2,128)(2,1)}, bf16[2,3,3,1,512]{4,0,2,1,3:T(2,128)(2,1)}, u32[]{:S(2)}, u32[]{:S(2)}) collective-permute-start(bf16[2,3,3,1,512]{4,0,2,1,3:T(2,128)(2,1)} %slice_bitcast_fusion.2), channel_id=1, source_target_pairs={{1,0},{2,1},{3,2},{4,3},{5,4},{6,5},{7,6},{8,7},{9,8},{10,9},{11,1... | collective-permute-start | bytes 55304 | tf_op jit(solution)/shard_map/ppermute | solution.py:263
  11.8 18.9 %collective-permute-start.1 = (bf16[256,3,1,2,512]{0,4,1,3,2:T(8,128)(2,1)}, bf16[256,3,1,2,512]{0,4,1,3,2:T(8,128)(2,1)}, u32[]{:S(2)}, u32[]{:S(2)}) collective-permute-start(bf16[256,3,1,2,512]{0,4,1,3,2:T(8,128)(2,1)} %bitcast.97), channel_id=1, source_target_pairs={{1,0},{2,1},{3,2},{4,3},{5,4},{6,5},{7,6},{8,7},{9,8},{10,9},{11,1... | collective-permute-start | bytes 4718600 | tf_op jit(solution)/shard_map/ppermute | solution.py:262
  17.6 0.7 copy-start.6
  17.7 0.9 copy-start.8
  17.7 0.9 copy-start.9
  17.8 2.8 %copy-start.5 = (f32[1,3,3,512]{3,0,2,1:T(1,128)S(1)}, f32[1,3,3,512]{3,0,2,1:T(1,128)}, u32[]{:S(2)}) copy-start(f32[1,3,3,512]{3,0,2,1:T(1,128)} %get-tuple-element.31) | copy-start | bytes 55300
  17.8 2.8 %copy-start.4 = (f32[1,3,3,512]{3,0,2,1:T(1,128)S(1)}, f32[1,3,3,512]{3,0,2,1:T(1,128)}, u32[]{:S(2)}) copy-start(f32[1,3,3,512]{3,0,2,1:T(1,128)} %get-tuple-element.32) | copy-start | bytes 55300
  17.8 2.8 %copy-start.3 = (f32[1,3,3,512]{3,0,2,1:T(1,128)S(1)}, f32[1,3,3,512]{3,0,2,1:T(1,128)}, u32[]{:S(2)}) copy-start(f32[1,3,3,512]{3,0,2,1:T(1,128)} %get-tuple-element.53) | copy-start | bytes 55300
  17.8 2.9 %copy-start.2 = (f32[1,3,3,512]{3,0,2,1:T(1,128)S(1)}, f32[1,3,3,512]{3,0,2,1:T(1,128)}, u32[]{:S(2)}) copy-start(f32[1,3,3,512]{3,0,2,1:T(1,128)} %get-tuple-element.54) | copy-start | bytes 55300
